TPU v7x, 8 devices: a whole 2x2x1 slice. The times are simulated.
8 devices in a mesh: data: 4 (over z, y, x), stage: 2 (over core).
Axes of the slice: x: 2, y: 2, z: 1, core: 2. Of those that a mesh axis runs over, the one named last changes fastest.
Arguments:
- w_up: float32 [2, 2, 1024, 4096], P(None, 'stage')
- w_down: float32 [2, 2, 4096, 1024], P(None, 'stage')
- m_up: float32 [2, 2, 1024, 4096], P(None, 'stage')
- m_down: float32 [2, 2, 4096, 1024], P(None, 'stage')
- v_up: float32 [2, 2, 1024, 4096], P(None, 'stage')
- v_down: float32 [2, 2, 4096, 1024], P(None, 'stage')
- g_up: float32 [4, 2, 2, 1024, 4096], P('data', None, 'stage')
- g_down: float32 [4, 2, 2, 4096, 1024], P('data', None, 'stage')
- act_stash: bfloat16 [2, 2, 3072, 1024], P(None, 'stage', 'data')
- dy_last: bfloat16 [3072, 1024], P('data')
- x_next: bfloat16 [16, 3072, 1024], P(None, 'data')
- max_norm: float32 [1], replicated
Outputs:
- output 1: float32 [2, 2, 1024, 4096], P(None, 'stage')
- output 2: float32 [2, 2, 4096, 1024], P(None, 'stage')
- output 3: float32 [2, 2, 1024, 4096], P(None, 'stage')
- output 4: float32 [2, 2, 4096, 1024], P(None, 'stage')
- output 5: float32 [2, 2, 1024, 4096], P(None, 'stage')
- output 6: float32 [2, 2, 4096, 1024], P(None, 'stage')
- output 7: bfloat16 [16, 3072, 1024], P(None, 'data')
All inputs are finite; a program needn't handle non-finite values.
Results may differ from a plain program's by a relative error of at most 0.00913332.
Values are sent between devices in bfloat16 or wider.
A program may use at most 2 GiB of HBM per device.

v0:
```python
import jax
import jax.numpy as jnp
from jax import lax
from jax.sharding import PartitionSpec as P

LR = 0.002
BETA1 = 0.9
BETA2 = 0.95
ADAM_EPS = 1e-8
WDECAY = 0.1
BIAS_ONE = 1.0 - BETA1 ** 10
BIAS_TWO = 1.0 - BETA2 ** 10
CONTRACT_ROWS = (((0,), (0,)), ((), ()))
CONTRACT_LAST = (((1,), (1,)), ((), ()))


def gelu_tanh(pre_act):
    return jax.nn.gelu(pre_act, approximate=True)


def layer_forward(act_in, w_in, w_out):
    pre_act = jnp.dot(act_in, w_in, preferred_element_type=jnp.float32)
    hidden = gelu_tanh(pre_act).astype(jnp.bfloat16)
    branch = jnp.dot(hidden, w_out, preferred_element_type=jnp.float32)
    return (act_in.astype(jnp.float32) + branch).astype(jnp.bfloat16)


def layer_backward(act_in, grad_y, w_in, w_out):
    pre_act = jnp.dot(act_in, w_in, preferred_element_type=jnp.float32)
    hidden, gelu_pull = jax.vjp(gelu_tanh, pre_act)
    hidden_b = hidden.astype(jnp.bfloat16)
    d_out = lax.dot_general(hidden_b, grad_y, CONTRACT_ROWS, preferred_element_type=jnp.float32)
    d_hid = lax.dot_general(grad_y, w_out, CONTRACT_LAST, preferred_element_type=jnp.float32)
    d_pre = gelu_pull(d_hid)[0].astype(jnp.bfloat16)
    d_in = lax.dot_general(act_in, d_pre, CONTRACT_ROWS, preferred_element_type=jnp.float32)
    back_rows = lax.dot_general(d_pre, w_in, CONTRACT_LAST, preferred_element_type=jnp.float32)
    grad_x = (grad_y.astype(jnp.float32) + back_rows).astype(jnp.bfloat16)
    return grad_x, d_in, d_out


def adamw_update(weight, mom, vel, grad):
    mom_new = BETA1 * mom + (1.0 - BETA1) * grad
    vel_new = BETA2 * vel + (1.0 - BETA2) * grad * grad
    step_dir = (mom_new / BIAS_ONE) / (jnp.sqrt(vel_new / BIAS_TWO) + ADAM_EPS)
    return weight - LR * (step_dir + WDECAY * weight), mom_new, vel_new


def solution(mesh):
    stages = mesh.shape['stage']
    replicas = mesh.shape['data']
    to_prev = [(src, (src - 1) % stages) for src in range(stages)]
    to_next = [(src, (src + 1) % stages) for src in range(stages)]
    w_spec = P(None, 'stage', None, None)
    g_spec = P('data', None, 'stage', None, None)
    s_spec = P(None, 'stage', 'data', None)
    dy_spec = P('data', None)
    x_spec = P(None, 'data', None)
    n_spec = P(None)

    def sharded(w_up, w_down, m_up, m_down, v_up, v_down, g_up, g_down, act_stash, dy_last, x_next, max_norm):
        stage_pos = lax.axis_index('stage')
        old_up = w_up[:, 0].astype(jnp.bfloat16)
        old_down = w_down[:, 0].astype(jnp.bfloat16)
        stash_rows = act_stash[:, 0]
        zero_in = jnp.zeros(old_up.shape[1:], jnp.float32)
        zero_out = jnp.zeros(old_down.shape[1:], jnp.float32)

        def back_layer(virtual, step_idx, carry):
            def run_layer(operands):
                return layer_backward(stash_rows[virtual], operands[0], old_up[virtual], old_down[virtual])
            def skip_layer(operands):
                return jnp.zeros_like(operands[0]), operands[1], operands[2]
            return lax.cond(stage_pos == stages - 1 - step_idx, run_layer, skip_layer, carry)

        def back_phase(virtual, grad_start, n_sends):
            def back_tick(step_idx, carry):
                grad_flow, acc_in, acc_out = back_layer(virtual, step_idx, carry)
                return lax.ppermute(grad_flow, 'stage', to_prev), acc_in, acc_out
            return lax.fori_loop(0, n_sends, back_tick, (grad_start, zero_in, zero_out))

        grad_flow, top_in, top_out = back_phase(1, dy_last, stages)
        grad_flow, low_in, low_out = back_phase(0, grad_flow, stages - 1)
        grad_flow, low_in, low_out = back_layer(0, stages - 1, (grad_flow, low_in, low_out))

        local_in = g_up[0, :, 0] + jnp.stack([low_in, top_in])
        local_out = g_down[0, :, 0] + jnp.stack([low_out, top_out])
        avg_in = lax.psum(local_in, 'data') / replicas
        avg_out = lax.psum(local_out, 'data') / replicas
        part_sq = jnp.sum(avg_in * avg_in) + jnp.sum(avg_out * avg_out)
        total_sq = lax.psum(part_sq, 'stage')
        clip_coef = jnp.minimum(1.0, max_norm[0] / (jnp.sqrt(total_sq) + 1e-6))
        new_up, mom_up, vel_up = adamw_update(w_up[:, 0], m_up[:, 0], v_up[:, 0], clip_coef * avg_in)
        new_down, mom_down, vel_down = adamw_update(w_down[:, 0], m_down[:, 0], v_down[:, 0], clip_coef * avg_out)
        fresh_up = new_up.astype(jnp.bfloat16)
        fresh_down = new_down.astype(jnp.bfloat16)

        n_micro = x_next.shape[0]
        n_ticks = n_micro + 2 * stages - 1

        def fwd_compute(tick_idx, act_slots, out_rows):
            made_slots = []
            for virtual in range(2):
                micro_idx = tick_idx - virtual * stages - stage_pos
                is_valid = (micro_idx >= 0) & (micro_idx < n_micro)
                def run_layer(act_in):
                    return layer_forward(act_in, fresh_up[virtual], fresh_down[virtual])
                made_slots.append(lax.cond(is_valid, run_layer, jnp.zeros_like, act_slots[virtual]))
            final_idx = tick_idx - stages - stage_pos
            is_final = (final_idx >= 0) & (final_idx < n_micro) & (stage_pos == stages - 1)
            safe_idx = jnp.clip(final_idx, 0, n_micro - 1)
            old_rows = lax.dynamic_index_in_dim(out_rows, safe_idx, 0, keepdims=False)
            out_rows = lax.dynamic_update_index_in_dim(out_rows, jnp.where(is_final, made_slots[1], old_rows), safe_idx, 0)
            return jnp.stack(made_slots), out_rows

        def fwd_tick(tick_idx, carry):
            act_slots, out_rows = carry
            made_slots, out_rows = fwd_compute(tick_idx, act_slots, out_rows)
            received = lax.ppermute(made_slots, 'stage', to_next)
            feed_rows = lax.dynamic_index_in_dim(x_next, jnp.minimum(tick_idx + 1, n_micro - 1), 0, keepdims=False)
            head_slots = jnp.stack([feed_rows, received[0]])
            return jnp.where(stage_pos == 0, head_slots, received), out_rows

        init_slots = jnp.stack([x_next[0], jnp.zeros_like(x_next[0])])
        act_slots = jnp.where(stage_pos == 0, init_slots, jnp.zeros_like(init_slots))
        act_slots, out_rows = lax.fori_loop(0, n_ticks - 1, fwd_tick, (act_slots, jnp.zeros_like(x_next)))
        act_slots, out_rows = fwd_compute(n_ticks - 1, act_slots, out_rows)
        y_next = lax.psum(jnp.where(stage_pos == stages - 1, out_rows, jnp.zeros_like(out_rows)), 'stage')
        return (new_up[:, None], new_down[:, None], mom_up[:, None], mom_down[:, None], vel_up[:, None], vel_down[:, None], y_next)

    return jax.shard_map(sharded, mesh=mesh, in_specs=(w_spec, w_spec, w_spec, w_spec, w_spec, w_spec, g_spec, g_spec, s_spec, dy_spec, x_spec, n_spec), out_specs=(w_spec, w_spec, w_spec, w_spec, w_spec, w_spec, x_spec), check_vma=False)
```

profile of v0, /device:TPU:0, one launch (start us, length us, event | category | flops | bytes accessed | tf_op | source)
XLA Modules:
  0.0 2770.8 jit_solution(2338665213877150761)
XLA Ops:
  57.2 143.9 %while.41 = (s32[]{:T(128)}, bf16[768,1024]{1,0:T(8,128)(2,1)S(1)}, f32[1024,4096]{0,1:T(8,128)}, f32[4096,1024]{1,0:T(8,128)}, s32[]{:T(128)}, /*index=5*/bf16[...) while((s32[]{:T(128)}, bf16[768,1024]{1,0:T(8,128)(2,1)S(1)}, ...), condition=%wide.region_3.0_spmd, body=%wide.region_0.0_spmd.sunk | while | flops 32305840128 | bytes 181403984 | solution.py:79
  57.6 68.7 %collective-permute-start = (bf16[768,1024]{1,0:T(8,128)(2,1)S(1)}, bf16[768,1024]{1,0:T(8,128)(2,1)S(1)}, u32[]{:S(2)}, u32[]{:S(2)}) collective-permute-start(bf16[768,1024]{1,0:T(8,128)(2,1)S(1)} %get-tuple-element.655), channel_id=1, source_target_pairs={{0,1},{1,0},{2,3},{3,2},{4,5},{5,4},{6,7},{7,6}} | collective-permute-start | bytes 4718600 | tf_op jit(solution)/shard_map/while/body/eval_jaxpr/ppermute | solution.py:78
  129.4 68.1 %conditional.12 = (bf16[768,1024]{1,0:T(8,128)(2,1)S(1)}, f32[1024,4096]{0,1:T(8,128)}, f32[4096,1024]{1,0:T(8,128)}) conditional(s32[]{:T(128)} %convert_element_type.155, (f32[1024,4096]{0,1:T(8,128)}, f32[4096,1024]{1,0:T(8,128)}) %tuple.141, (bf16[768,1024]{1,0:T(8,128)(2,1)S(1)}, bf16[2,4096,1024]{2,1,0:T(8,128)(2,1)}, ...), branch_computations={%region_1.0_spmd, %region_2.0_spmd} | conditional | flops 32305840128 | bytes 175112320 | solution.py:73
  223.5 59.5 %collective-permute-start.2 = (bf16[768,1024]{1,0:T(8,128)(2,1)S(1)}, bf16[768,1024]{1,0:T(8,128)(2,1)S(1)}, u32[]{:S(2)}, u32[]{:S(2)}) collective-permute-start(bf16[768,1024]{1,0:T(8,128)(2,1)S(1)} %get-tuple-element.498), channel_id=1, source_target_pairs={{0,1},{1,0},{2,3},{3,2},{4,5},{5,4},{6,7},{7,6}} | collective-permute-start | bytes 4718600 | tf_op jit(solution)/shard_map/while/body/eval_jaxpr/ppermute | solution.py:78
  300.4 52.4 %conditional.7 = (f32[4096,1024]{1,0:T(8,128)}, f32[1024,4096]{0,1:T(8,128)}) conditional(s32[]{:T(128)} %convert_element_type.106, (f32[1024,4096]{0,1:T(8,128)}, f32[4096,1024]{1,0:T(8,128)}) %tuple.104, (bf16[2,4096,1024]{2,1,0:T(8,128)(2,1)}, bf16[768,1024]{1,0:T(8,128)(2,1)S(1)}, bf16[2,768,1024]{2,1,0:T(8,128)(2,1)}, ...), branch_computations={%region_6.7_spmd, %region_7.0_spmd} | conditional | flops 25861029888 | bytes 163577968 | solution.py:73
  326.2 26.2 convolution_bitcast_fusion.2
  370.3 33.5 %maximum_add_fusion = f32[2,1024,4096]{2,1,0:T(8,128)} fusion(f32[1,1024,4096]{2,1,0:T(8,128)} %bitcast.245, f32[1,1024,4096]{2,1,0:T(8,128)} %bitcast.247, f32[1,2,1,1024,4096]{4,3,2,1,0:T(8,128)} %param.34), kind=kLoop, calls=%fused_computation.181 | loop fusion | flops 16777216 | bytes 100663296 | tf_op jit(solution)/shard_map/add | solution.py:85
  403.8 33.2 %maximum_add_fusion.1 = f32[2,4096,1024]{2,1,0:T(8,128)} fusion(f32[1,4096,1024]{2,1,0:T(8,128)} %bitcast.246, f32[1,4096,1024]{2,1,0:T(8,128)} %bitcast.35, f32[1,2,1,4096,1024]{4,3,2,1,0:T(8,128)} %param.35), kind=kLoop, calls=%fused_computation.182 | loop fusion | flops 16777216 | bytes 100663296 | tf_op jit(solution)/shard_map/add | solution.py:86
  441.7 1102.5 %all-reduce.6.cloned.1.call-done = (f32[2,1024,4096]{2,1,0:T(8,128)}, f32[2,4096,1024]{2,1,0:T(8,128)}) async-done(((f32[2,1024,4096]{2,1,0:T(8,128)}, f32[2,4096,1024]{2,1,0:T(8,128)}), (f32[2,1024,4096]{2,1,0:T(8,128)}, f32[2,4096,1024]{2,1,0:T(8,128)})) %all-reduce.6.cloned.1.call-update) | async-done | bytes 67108880 | tf_op jit(solution)/shard_map/psum | solution.py:87
  1578.6 81.0 %fusion.205 = (bf16[2,1024,4096]{2,1,0:T(8,128)(2,1)}, f32[2,1024,4096]{2,1,0:T(8,128)}, f32[2,1,1024,4096]{3,2,1,0:T(8,128)}, f32[2,1,1024,4096]{3,2,1,0:T(8,128)}) fusion(f32[2,1,1024,4096]{3,2,1,0:T(8,128)} %param.32, f32[2,1024,4096]{2,1,0:T(8,128)} %get-tuple-element.541, f32[]{:T(128)S(6)} %mul.262, f32[2,1,1024,4096]{3,2,1,0:T(8,128)} %param.30, ...), kind=kLoop, calls=%fused_computation.211 | loop fusion | flops 142606336 | bytes 251658240 | tf_op jit(solution)/shard_map/convert_element_type | solution.py:94
  1659.6 84.5 %fusion.204 = (bf16[2,4096,1024]{2,1,0:T(8,128)(2,1)}, f32[2,4096,1024]{2,1,0:T(8,128)}, f32[2,1,4096,1024]{3,2,1,0:T(8,128)}, f32[2,1,4096,1024]{3,2,1,0:T(8,128)}) fusion(f32[2,1,4096,1024]{3,2,1,0:T(8,128)} %param.33, f32[2,4096,1024]{2,1,0:T(8,128)} %get-tuple-element.542, f32[]{:T(128)S(6)} %mul.262, f32[2,1,4096,1024]{3,2,1,0:T(8,128)} %param.31, ...), kind=kLoop, calls=%fused_computation.210 | loop fusion | flops 142606336 | bytes 251658240 | tf_op jit(solution)/shard_map/convert_element_type | solution.py:95
  1752.8 877.9 %while.42 = (s32[]{:T(128)}, bf16[2,768,1024]{2,1,0:T(8,128)(2,1)}, bf16[16,768,1024]{2,1,0:T(8,128)(2,1)}, pred[]{:T(512)}, bf16[16,768,1024]{2,1,0:T(8,128)(2,...) while((s32[]{:T(128)}, bf16[2,768,1024]{2,1,0:T(8,128)(2,1)}, ...), condition=%wide.region_18.0_spmd, body=%wide.region_13.18_spmd.sunk | while | flops 25836650496 | bytes 88605072 | solution.py:125
  1754.5 19.9 conditional.14
  1754.5 19.9 fusion.127
  1785.8 19.9 conditional.14
  1785.8 19.9 fusion.127
  1815.5 22.5 conditional.13
  1815.5 21.1 add_convert_fusion.3
  1838.0 19.9 conditional.14
  1838.0 19.9 fusion.127
  1867.7 22.5 conditional.13
  1867.7 21.1 add_convert_fusion.3
  1890.2 19.9 conditional.14
  1890.2 19.9 fusion.127
  1919.9 22.5 conditional.13
  1919.9 21.1 add_convert_fusion.3
  1972.1 22.5 conditional.13
  1972.1 21.1 add_convert_fusion.3
  1994.6 19.9 conditional.14
  2024.3 22.5 conditional.13
  2024.3 21.1 add_convert_fusion.3
  2076.4 22.5 conditional.13
  2076.4 21.1 add_convert_fusion.3
  2098.9 19.9 conditional.14
  2098.9 19.9 fusion.127
  2128.6 22.5 conditional.13
  2128.6 21.1 add_convert_fusion.3
  2180.8 22.5 conditional.13
  2180.8 21.1 add_convert_fusion.3
  2203.3 19.9 conditional.14
  2203.3 19.9 fusion.127
  2233.0 22.5 conditional.13
  2233.0 21.1 add_convert_fusion.3
  2285.2 22.5 conditional.13
  2285.2 21.1 add_convert_fusion.3
  2307.6 19.9 conditional.14
  2307.6 19.9 fusion.127
  2337.3 22.5 conditional.13
  2337.3 21.1 add_convert_fusion.3
  2389.5 22.5 conditional.13
  2389.5 21.1 add_convert_fusion.3
  2412.0 19.9 conditional.14
  2441.7 22.5 conditional.13
  2441.7 21.1 add_convert_fusion.3
  2493.9 22.5 conditional.13
  2493.9 21.1 add_convert_fusion.3
  2516.4 19.9 conditional.14
  2516.4 19.9 fusion.127
  2546.1 22.5 conditional.13
  2546.1 21.1 add_convert_fusion.3
  2598.0 22.5 conditional.13
  2598.0 21.1 add_convert_fusion.3
  2643.7 99.2 %all-reduce.4.cloned.1.call-done = bf16[16,768,1024]{2,1,0:T(8,128)(2,1)} async-done(((bf16[16,768,1024]{2,1,0:T(8,128)(2,1)}), bf16[16,768,1024]{2,1,0:T(8,128)(2,1)}) %all-reduce.4.cloned.1.call-update) | async-done | bytes 25165840 | tf_op jit(solution)/shard_map/psum | solution.py:127
  2742.9 20.7 copy.78
  (228 shorter events, 769.8 us)
Async XLA Ops:
  7.2 1537.0 %all-reduce.6.cloned.1.call-start = ((), (), s32[]{:S(2)}) async-start(), calls=%async_computation.1 | async-start | bytes 134217728 | tf_op jit(solution)/shard_map/psum | solution.py:87
  7.2 26.2 copy-start
  48.9 8.3 copy-start.2
  57.6 71.8 %collective-permute-start = (bf16[768,1024]{1,0:T(8,128)(2,1)S(1)}, bf16[768,1024]{1,0:T(8,128)(2,1)S(1)}, u32[]{:S(2)}, u32[]{:S(2)}) collective-permute-start(bf16[768,1024]{1,0:T(8,128)(2,1)S(1)} %get-tuple-element.655), channel_id=1, source_target_pairs={{0,1},{1,0},{2,3},{3,2},{4,5},{5,4},{6,7},{7,6}} | collective-permute-start | bytes 4718600 | tf_op jit(solution)/shard_map/while/body/eval_jaxpr/ppermute | solution.py:78
  160.7 11.2 copy-start.4
  160.7 24.5 slice-start
  160.7 24.5 slice-start.1
  171.9 13.3 slice-start.2
  197.4 3.4 collective-permute-start
  209.4 8.3 copy-start.5
  223.5 77.0 %collective-permute-start.2 = (bf16[768,1024]{1,0:T(8,128)(2,1)S(1)}, bf16[768,1024]{1,0:T(8,128)(2,1)S(1)}, u32[]{:S(2)}, u32[]{:S(2)}) collective-permute-start(bf16[768,1024]{1,0:T(8,128)(2,1)S(1)} %get-tuple-element.498), channel_id=1, source_target_pairs={{0,1},{1,0},{2,3},{3,2},{4,5},{5,4},{6,7},{7,6}} | collective-permute-start | bytes 4718600 | tf_op jit(solution)/shard_map/while/body/eval_jaxpr/ppermute | solution.py:78
  300.4 1.2 copy-start.7
  311.2 15.0 copy-start.8
  311.2 15.0 copy-start.6
  437.0 0.7 copy-start.3
  437.0 2305.9 %all-reduce.4.cloned.1.call-start = ((), (), s32[]{:S(2)}) async-start(), calls=%async_computation | async-start | bytes 50331648 | tf_op jit(solution)/shard_map/psum | solution.py:127
  1544.1 20.2 copy-start.1
  1776.4 5.7 collective-permute-start.1
  1807.7 5.7 collective-permute-start.1
  1859.8 5.7 collective-permute-start.1
  1912.0 5.7 collective-permute-start.1
  1964.2 5.7 collective-permute-start.1
  2016.4 5.7 collective-permute-start.1
  2068.6 5.7 collective-permute-start.1
  2120.8 5.7 collective-permute-start.1
  2172.9 5.7 collective-permute-start.1
  2225.1 5.7 collective-permute-start.1
  2277.3 5.7 collective-permute-start.1
  2329.5 5.7 collective-permute-start.1
  2381.7 5.7 collective-permute-start.1
  2433.8 5.7 collective-permute-start.1
  2486.0 5.7 collective-permute-start.1
  2538.2 5.7 collective-permute-start.1
  2570.7 25.2 collective-permute-start.1
  2622.6 5.7 collective-permute-start.1
Sparse Core Ops, SparseCore 0:
  437.2 1106.9 all-reduce.5
  2643.8 99.0 all-reduce.3
where the time goes:
time: 2780 us; the launch traced here: 2770 us
  waiting for transfers between devices  1220 us (44%)
  matrix products  774 us (28%)
  other arithmetic  429 us (15%)
  local copies, waits for them, and re-layouts  169 us (6%)
  starting transfers between devices  151 us (5%)
    psum x1, waiting for transfers between devices, sharded(): avg_in = lax.psum(local_in, 'data') / replicas  1100 us
    dot_general x32, matrix products, layer_forward(): branch = jnp.dot(hidden, w_out, preferred_element_type=jnp.float32)  656 us
    ppermute x3, starting transfers between devices, back_tick(): return (lax.ppermute(grad_flow, 'stage', to_prev), acc_in, acc_out)  128 us
    psum x1, waiting for transfers between devices, sharded(): lax.psum(jnp.where(stage_pos == stages - 1, out_rows, jnp.zeros_like(out_...  99.2 us
    convert_element_type x1, other arithmetic, sharded(): fresh_down = new_down.astype(jnp.bfloat16)  84.5 us
    convert_element_type x1, other arithmetic, sharded(): fresh_up = new_up.astype(jnp.bfloat16)  81 us
    dynamic_update_slice x19, other arithmetic, fwd_compute(): lax.dynamic_update_index_in_dim(out_rows, jnp.where(is_final, made_slots[...  61.4 us
  transfers between devices with their start and end apart: 23, of which 22 were waited for; matrix products, arithmetic and copies ran while one was open for 4% of the time, Pallas kernels for 0%

commit v1 on v0

v1 whole, which is shorter than its diff:
```python
import functools

import jax
import jax.numpy as jnp
from jax import lax
from jax.experimental import pallas as pl
from jax.experimental.pallas import tpu as pltpu
from jax.sharding import PartitionSpec as P

LR = 0.002
BETA1 = 0.9
BETA2 = 0.95
ADAM_EPS = 1e-8
WDECAY = 0.1
BIAS_ONE = 1.0 - BETA1 ** 10
BIAS_TWO = 1.0 - BETA2 ** 10
CONTRACT_ROWS = (((0,), (0,)), ((), ()))
CONTRACT_LAST = (((1,), (1,)), ((), ()))
F32 = jnp.float32
BF16 = jnp.bfloat16


def gelu_tanh(pre_act):
    return jax.nn.gelu(pre_act, approximate=True)


def adamw_update(weight, mom, vel, grad):
    mom_new = BETA1 * mom + (1.0 - BETA1) * grad
    vel_new = BETA2 * vel + (1.0 - BETA2) * grad * grad
    step_dir = (mom_new / BIAS_ONE) / (jnp.sqrt(vel_new / BIAS_TWO) + ADAM_EPS)
    return weight - LR * (step_dir + WDECAY * weight), mom_new, vel_new


def adamw_body(clip, w, m, v, g, *rest):
    w_out, m_out, v_out, b_out = rest[-4:]
    new_w, new_m, new_v = adamw_update(w[0, 0], m[0, 0], v[0, 0], clip[0] * g[...])
    w_out[0, 0] = new_w
    m_out[0, 0] = new_m
    v_out[0, 0] = new_v
    b_out[...] = new_w.astype(BF16)


def adamw_call(virtual, clip, w, m, v, grad, prev):
    rows, cols = grad.shape
    block = 262144 // cols
    big = pl.BlockSpec((1, 1, block, cols), lambda i: (virtual, 0, i, 0))
    flat = pl.BlockSpec((block, cols), lambda i: (i, 0))
    in_specs = [pl.BlockSpec(memory_space=pltpu.SMEM), big, big, big, flat]
    args = [clip, w, m, v, grad]
    aliases = {}
    if prev is not None:
        in_specs += [pl.BlockSpec(memory_space=pl.ANY)] * 3
        args += list(prev)
        aliases = {5: 0, 6: 1, 7: 2}
    like = jax.ShapeDtypeStruct(w.shape, F32)
    return pl.pallas_call(
        adamw_body,
        grid=(rows // block,),
        in_specs=in_specs,
        out_specs=[big, big, big, flat],
        out_shape=[like, like, like, jax.ShapeDtypeStruct((rows, cols), BF16)],
        input_output_aliases=aliases,
        cost_estimate=pl.CostEstimate(flops=20 * rows * cols, bytes_accessed=30 * rows * cols, transcendentals=0),
        compiler_params=pltpu.CompilerParams(vmem_limit_bytes=40 * 1024 * 1024),
        name="adamw",
    )(*args)


def solution(mesh):
    replicas = mesh.shape['data']
    down_hop, up_hop, swap = [(1, 0)], [(0, 1)], [(0, 1), (1, 0)]
    w_spec = P(None, 'stage', None, None)
    g_spec = P('data', None, 'stage', None, None)
    s_spec = P(None, 'stage', 'data', None)
    dy_spec = P('data', None)
    x_spec = P(None, 'data', None)
    n_spec = P(None)

    def sharded(w_up, w_down, m_up, m_down, v_up, v_down, g_up, g_down, act_stash, dy_last, x_next, max_norm):
        pos = lax.axis_index('stage')
        rep = lax.axis_index('data')
        old_up = [w_up[v, 0].astype(BF16) for v in range(2)]
        old_down = [w_down[v, 0].astype(BF16) for v in range(2)]
        stash = [act_stash[v, 0] for v in range(2)]

        def pre_hidden(v):
            pre_act = jnp.dot(stash[v], old_up[v], preferred_element_type=F32)
            return pre_act, gelu_tanh(pre_act).astype(BF16)

        def chain(v, pre_act, grad_y):
            d_hid = lax.dot_general(grad_y, old_down[v], CONTRACT_LAST, preferred_element_type=F32)
            d_pre = jax.vjp(gelu_tanh, pre_act)[1](d_hid)[0].astype(BF16)
            back_rows = lax.dot_general(d_pre, old_up[v], CONTRACT_LAST, preferred_element_type=F32)
            return d_pre, (grad_y.astype(F32) + back_rows).astype(BF16)

        def backward(v, grad_top):
            pre_act, hidden = pre_hidden(v)
            zeros = (jnp.zeros(hidden.shape, BF16), jnp.zeros(grad_top.shape, BF16))
            first = lax.cond(pos == 1, lambda g: chain(v, pre_act, g), lambda g: zeros, grad_top)
            grad_mid = lax.ppermute(first[1], 'stage', down_hop)
            d_pre, grad_bottom = lax.cond(pos == 0, lambda g: chain(v, pre_act, g), lambda g: first, grad_mid)
            grad_y = jnp.where(pos == 1, grad_top, grad_mid)
            sum_down = lax.dot_general(hidden, grad_y, CONTRACT_ROWS, preferred_element_type=F32) + g_down[0, v, 0]
            part_down = lax.psum_scatter(sum_down, 'data', scatter_dimension=0, tiled=True)
            sum_up = lax.dot_general(stash[v], d_pre, CONTRACT_ROWS, preferred_element_type=F32) + g_up[0, v, 0]
            part_up = lax.psum_scatter(sum_up, 'data', scatter_dimension=0, tiled=True)
            return lax.ppermute(grad_bottom, 'stage', up_hop), part_up, part_down

        grad_flow, up1, down1 = backward(1, dy_last)
        grad_flow, up0, down0 = backward(0, grad_flow)
        up = [up0 / replicas, up1 / replicas]
        down = [down0 / replicas, down1 / replicas]

        part_sq = sum(jnp.sum(t * t) for t in up + down)
        total_sq = lax.psum(part_sq, ('data', 'stage'))
        clip = jnp.minimum(1.0, max_norm / (jnp.sqrt(total_sq) + 1e-6))

        def gather(t):
            return lax.all_gather(t, 'data', axis=0, tiled=True)

        def shard(t, like):
            rows = like.shape[0]
            return lax.dynamic_slice_in_dim(t[0, 0], rep * rows, rows, 0)

        def fresh_shard(w, m, v, grad):
            return adamw_update(shard(w, grad), shard(m, grad), shard(v, grad), clip[0] * grad)[0].astype(BF16)

        def both(t):
            other = lax.ppermute(t, 'stage', swap)
            return jnp.where(pos == 0, t, other), jnp.where(pos == 0, other, t)

        def forward(act, w_in, w_out):
            pre_act = jnp.dot(act, w_in, preferred_element_type=F32)
            hidden = gelu_tanh(pre_act).astype(BF16)
            branch = jnp.dot(hidden, w_out, preferred_element_type=F32)
            return (act.astype(F32) + branch).astype(BF16)

        n_micro, rows, width = x_next.shape
        half = n_micro // 2
        act = lax.dynamic_slice_in_dim(x_next, pos * half, half, 0).reshape(half * rows, width)

        full_down1 = gather(down[1])
        fresh_up0 = gather(fresh_shard(w_up, m_up, v_up, up[0]))
        fresh_down0 = gather(fresh_shard(w_down, m_down, v_down, down[0]))
        full_up1 = gather(up[1])
        pair_up, pair_down = both(fresh_up0), both(fresh_down0)
        for l in range(2):
            act = forward(act, pair_up[l], pair_down[l])

        *new_down, fresh_down1 = adamw_call(1, clip, w_down, m_down, v_down, full_down1, None)
        *new_up, fresh_up1 = adamw_call(1, clip, w_up, m_up, v_up, full_up1, None)
        pair_up, pair_down = both(fresh_up1), both(fresh_down1)
        full_down0 = gather(down[0])
        full_up0 = gather(up[0])
        for l in range(2):
            act = forward(act, pair_up[l], pair_down[l])
        *new_down, _ = adamw_call(0, clip, w_down, m_down, v_down, full_down0, new_down)
        *new_up, _ = adamw_call(0, clip, w_up, m_up, v_up, full_up0, new_up)

        own = act.reshape(half, rows, width)
        other = lax.ppermute(own, 'stage', swap)
        y_next = jnp.where(pos == 0, jnp.concatenate([own, other]), jnp.concatenate([other, own]))
        return (new_up[0], new_down[0], new_up[1], new_down[1], new_up[2], new_down[2], y_next)

    return jax.shard_map(sharded, mesh=mesh, in_specs=(w_spec, w_spec, w_spec, w_spec, w_spec, w_spec, g_spec, g_spec, s_spec, dy_spec, x_spec, n_spec), out_specs=(w_spec, w_spec, w_spec, w_spec, w_spec, w_spec, x_spec), check_vma=False)
```

time: 2780 us -> 1700 us (0.61)
  waiting for transfers between devices: 1220 us -> 595 us
  other arithmetic: 429 us -> 62.6 us
  Pallas kernels: 0 us -> 180 us
  starting transfers between devices: 151 us -> 7.32 us
  matrix products: 774 us -> 696 us
  local copies, waits for them, and re-layouts: 169 us -> 114 us
    psum x2 -> x0, waiting for transfers between devices: 1200 us -> none  [the longest x1 1100 us: sharded(): avg_in = lax.psum(local_in, 'data') / replicas]
    reduce_scatter x0 -> x4, waiting for transfers between devices: none -> 439 us  [the longest x2 292 us: backward(): lax.psum_scatter(sum_down, 'data', scatter_dimension=0, tiled=True)]
    pallas_call x0 -> x4, Pallas kernels: none -> 180 us  [adamw_call(): pl.pallas_call(adamw_body, grid=(rows // block,), in_specs=in_specs, out_...]
    convert_element_type x4 -> x2, other arithmetic: 191 us -> 18.6 us  [fresh_shard(): adamw_update(shard(w, grad), shard(m, grad), shard(v, grad), clip[0] * grad)]
    ppermute x21 -> x8, starting transfers between devices: 151 us -> 6.33 us  [the longest x1 2.72 us: backward(): return (lax.ppermute(grad_bottom, 'stage', up_hop), part_up, part_down)]
    all_gather x0 -> x6, waiting for transfers between devices: none -> 109 us  [gather(): return lax.all_gather(t, 'data', axis=0, tiled=True)]
    dot_general x40 -> x17, matrix products: 774 us -> 696 us  [the longest x4 305 us: forward(): pre_act = jnp.dot(act, w_in, preferred_element_type=F32)]
    slice x18 -> x6, local copies, waits for them, and re-layouts: 2.15 us -> 71.2 us  [the longest x4 47.4 us: shard(): return lax.dynamic_slice_in_dim(t[0, 0], rep * rows, rows, 0)]
  transfers between devices with their start and end apart: 23 -> 18, of which waited for: 22 -> 8; matrix products, arithmetic and copies ran while one was open for 4% -> 44% of each run, Pallas kernels for 0% -> 11%
where the time goes in v1:
time: 1700 us
  matrix products  696 us (41%)
  waiting for transfers between devices  595 us (35%)
  Pallas kernels  180 us (11%)
  local copies, waits for them, and re-layouts  114 us (7%)
  other arithmetic  62.6 us (4%)
  blocking collectives  22.2 us (1%)
  between operations  18.5 us (1%)
    dot_general x4, matrix products, forward(): pre_act = jnp.dot(act, w_in, preferred_element_type=F32)  305 us
    reduce_scatter x2, waiting for transfers between devices, backward(): lax.psum_scatter(sum_down, 'data', scatter_dimension=0, tiled=True)  292 us
    dot_general x4, matrix products, forward(): branch = jnp.dot(hidden, w_out, preferred_element_type=F32)  242 us
    pallas_call x4, Pallas kernels, adamw_call(): pl.pallas_call(adamw_body, grid=(rows // block,), in_specs=in_specs, out_...  180 us
    reduce_scatter x2, waiting for transfers between devices, backward(): part_up = lax.psum_scatter(sum_up, 'data', scatter_dimension=0, tiled=True)  147 us
    all_gather x6, waiting for transfers between devices, gather(): return lax.all_gather(t, 'data', axis=0, tiled=True)  109 us
    slice x4, local copies, waits for them, and re-layouts, shard(): return lax.dynamic_slice_in_dim(t[0, 0], rep * rows, rows, 0)  47.4 us
    ppermute x2, waiting for transfers between devices, backward(): grad_mid = lax.ppermute(first[1], 'stage', down_hop)  44.3 us
  transfers between devices with their start and end apart: 18, of which 8 were waited for; matrix products, arithmetic and copies ran while one was open for 44% of the time, Pallas kernels for 11%

profile of v1, /device:TPU:0, one launch (start us, length us, event | category | flops | bytes accessed | tf_op | source)
XLA Modules:
  0.0 1696.1 jit_solution(3553439208394747938)
XLA Ops:
  7.2 17.9 %convert_bitcast_fusion = (bf16[4096,1024]{1,0:T(8,128)(2,1)}, bf16[4096,1024]{1,0:T(8,128)(2,1)}) fusion(f32[2,1,4096,1024]{3,2,1,0:T(8,128)} %w.7), kind=kLoop, calls=%fused_computation.123 | loop fusion | bytes 33554432 | tf_op jit(solution)/shard_map/convert_element_type | solution.py:83
  25.1 6.6 fusion.81
  31.9 18.0 %fusion.140 = f32[768,4096]{1,0:T(8,128)} fusion(bf16[2,1,768,1024]{3,2,1,0:T(8,128)(2,1)S(1)} %copy-done.2, f32[2,1,1024,4096]{3,2,1,0:T(8,128)} %w.5), kind=kOutput, calls=%fused_computation.175 | convolution fusion | flops 6442450944 | bytes 22544384 | tf_op jit(solution)/shard_map/dot_general | solution.py:87
  49.9 3.7 conditional.4
  49.9 3.5 broadcast.94
  53.4 0.2 broadcast.95
  53.5 1.3 collective-permute-start
  54.9 27.0 %collective-permute-done = bf16[768,1024]{1,0:T(8,128)(2,1)} collective-permute-done((bf16[768,1024]{1,0:T(8,128)(2,1)S(1)}, bf16[768,1024]{1,0:T(8,128)(2,1)}, u32[]{:S(2)}, u32[]{:S(2)}) %collective-permute-start) | collective-permute-done | bytes 1572896 | tf_op jit(solution)/shard_map/ppermute | solution.py:100
  81.9 29.3 %conditional.5 = ((bf16[768,4096]{1,0:T(8,128)(2,1)}, bf16[768,1024]{1,0:T(8,128)(2,1)S(1)})) conditional(s32[]{:T(128)} %convert_element_type.115, (bf16[768,4096]{1,0:T(8,128)(2,1)}, bf16[768,1024]{1,0:T(8,128)(2,1)S(1)}) %conditional.4, (bf16[768,1024]{1,0:T(8,128)(2,1)}, bf16[4096,1024]{1,0:T(8,128)(2,1)}, f32[768,4096]{1,0:T(8,128)}, ...), branch_computations={%region_2.0_spmd, %region_3.0_spmd} | conditional | flops 12950175744 | bytes 80216120 | solution.py:101
  82.4 19.6 %fusion.13 = bf16[768,4096]{1,0:T(8,128)(2,1)} fusion(f32[768,4096]{1,0:T(8,128)} %get-tuple-element.47, bf16[768,1024]{1,0:T(8,128)(2,1)} %get-tuple-element.45, bf16[4096,1024]{1,0:T(8,128)(2,1)} %get-tuple-element.46), kind=kOutput, calls=%fused_computation.18 | convolution fusion | flops 6505365504 | bytes 28835840 | tf_op jit(solution)/shard_map/cond/branch_1_fun/dot_general | solution.py:91
  102.1 9.0 add_convert_fusion.1
  111.2 15.2 bitcast_add_fusion.2
  126.5 18.1 %bitcast_add_fusion = f32[4096,1024]{1,0:T(8,128)} fusion(f32[1,2,1,4096,1024]{4,3,2,1,0:T(8,128)} %param.27, f32[768,4096]{1,0:T(8,128)} %fusion.140, bf16[768,1024]{1,0:T(8,128)(2,1)S(1)} %copy-done.5, bf16[768,1024]{1,0:T(8,128)(2,1)} %collective-permute-done, pred[]{:T(512)S(6)} %eq.5), kind=kOutput, calls=%fused_computation.86 | convolution fusion | flops 6475743232 | bytes 49283072 | tf_op jit(solution)/shard_map/dot_general | solution.py:103
  144.7 11.9 slice.50
  156.6 2.7 collective-permute-start.1
  159.3 15.2 fusion.83
  174.5 3.9 conditional.6
  174.5 0.2 broadcast.106
  174.7 3.5 broadcast.107
  178.4 1.3 collective-permute-start.2
  179.7 17.3 %collective-permute-done.2 = bf16[768,1024]{1,0:T(8,128)(2,1)} collective-permute-done((bf16[768,1024]{1,0:T(8,128)(2,1)S(1)}, bf16[768,1024]{1,0:T(8,128)(2,1)}, u32[]{:S(2)}, u32[]{:S(2)}) %collective-permute-start.2) | collective-permute-done | bytes 1572896 | tf_op jit(solution)/shard_map/ppermute | solution.py:100
  197.0 20.1 %conditional.7 = (bf16[768,4096]{1,0:T(8,128)(2,1)}) conditional(s32[]{:T(128)} %convert_element_type.115, bf16[768,4096]{1,0:T(8,128)(2,1)} %get-tuple-element.84, (bf16[768,1024]{1,0:T(8,128)(2,1)}, bf16[4096,1024]{1,0:T(8,128)(2,1)}, f32[768,4096]{1,0:T(8,128)}) %tuple.45), branch_computations={%region_6.7_spmd, %region_7.8_spmd} | conditional | flops 6505365504 | bytes 28835848 | solution.py:101
  197.4 19.7 %fusion.32 = bf16[768,4096]{1,0:T(8,128)(2,1)} fusion(f32[768,4096]{1,0:T(8,128)} %get-tuple-element.55, bf16[768,1024]{1,0:T(8,128)(2,1)} %get-tuple-element.53, bf16[4096,1024]{1,0:T(8,128)(2,1)} %get-tuple-element.54), kind=kOutput, calls=%fused_computation.41 | convolution fusion | flops 6505365504 | bytes 28835840 | tf_op jit(solution)/shard_map/cond/branch_1_fun/dot_general | solution.py:91
  217.1 15.7 bitcast_add_fusion.3
  232.8 0.2 reduce-scatter.9.cloned.1.call-start
  233.0 18.1 %bitcast_add_fusion.1 = f32[4096,1024]{1,0:T(8,128)} fusion(f32[1,2,1,4096,1024]{4,3,2,1,0:T(8,128)} %param.27, f32[768,4096]{1,0:T(8,128)} %fusion.83, bf16[768,1024]{1,0:T(8,128)(2,1)} %collective-permute-done.1, bf16[768,1024]{1,0:T(8,128)(2,1)} %collective-permute-done.2, pred[]{:T(512)S(6)} %eq.5), kind=kOutput, calls=%fused_computation.87 | convolution fusion | flops 6475743232 | bytes 49283072 | tf_op jit(solution)/shard_map/dot_general | solution.py:103
  251.9 11.7 slice.56
  263.6 11.7 slice.55
  275.3 1.0 reduce-scatter.7.cloned.1.call-done
  276.4 5.8 broadcast_multiply_fusion.2
  282.2 145.7 %reduce-scatter.11.cloned.1.call-done = f32[1024,1024]{1,0:T(8,128)} async-done(((f32[4096,1024]{1,0:T(8,128)}), f32[1024,1024]{1,0:T(8,128)}) %reduce-scatter.11.cloned.1.call-update) | async-done | bytes 4194320 | tf_op jit(solution)/shard_map/reduce_scatter | solution.py:104
  427.9 5.9 broadcast_multiply_fusion
  433.8 145.7 %reduce-scatter.5.cloned.1.call-done = f32[256,4096]{1,0:T(8,128)} async-done(((f32[1024,4096]{1,0:T(8,128)}), f32[256,4096]{1,0:T(8,128)}) %reduce-scatter.5.cloned.1.call-update) | async-done | bytes 4194320 | tf_op jit(solution)/shard_map/reduce_scatter | solution.py:106
  579.5 3.9 multiply_reduce_fusion.3
  584.7 146.2 %reduce-scatter.9.cloned.1.call-done = f32[1024,1024]{1,0:T(8,128)} async-done(((f32[4096,1024]{1,0:T(8,128)}), f32[1024,1024]{1,0:T(8,128)}) %reduce-scatter.9.cloned.1.call-update) | async-done | bytes 4194320 | tf_op jit(solution)/shard_map/reduce_scatter | solution.py:104
  730.9 3.9 multiply_reduce_fusion.1
  736.1 22.2 %psum.7 = f32[]{:T(128)} all-reduce(f32[]{:T(128)S(6)} %add.172), channel_id=1, replica_groups=mesh['data'=4,'stage'=2] {'data','stage'}, use_global_device_ids=true, to_apply=%region_16.17 | all-reduce | flops 1 | bytes 8 | tf_op jit(solution)/shard_map/psum | solution.py:115
  759.1 9.2 fusion.136
  768.3 0.4 all-gather.17.cloned.1.call-start
  768.8 12.0 slice.48
  780.7 12.0 slice.58
  792.7 12.0 slice.57
  804.7 9.3 fusion.134
  814.1 0.7 all-gather.9.cloned.1.call-update
  814.8 0.7 all-gather.13.cloned.1.call-update
  815.6 0.7 all-gather.7.cloned.1.call-update
  816.3 35.9 %all-gather.15.cloned.1.call-done = bf16[1024,4096]{1,0:T(8,128)(2,1)} async-done(((bf16[256,4096]{1,0:T(8,128)(2,1)}), bf16[1024,4096]{1,0:T(8,128)(2,1)}) %all-gather.15.cloned.1.call-update) | async-done | bytes 8388624 | tf_op jit(solution)/shard_map/all_gather | solution.py:119
  852.2 10.5 constant_dynamic-slice_fusion
  862.8 73.5 %all-gather.17.cloned.1.call-done = bf16[4096,1024]{1,0:T(8,128)(2,1)} async-done(((bf16[1024,1024]{1,0:T(8,128)(2,1)}), bf16[4096,1024]{1,0:T(8,128)(2,1)}) %all-gather.17.cloned.1.call-update) | async-done | bytes 8388624 | tf_op jit(solution)/shard_map/all_gather | solution.py:119
  936.3 76.2 %fusion.40 = bf16[6144,4096]{1,0:T(8,128)(2,1)} fusion(bf16[6144,1024]{1,0:T(8,128)(2,1)} %bitcast.110, bf16[1024,4096]{1,0:T(8,128)(2,1)} %all-gather.15.cloned.1.call-done, bf16[1024,4096]{1,0:T(8,128)(2,1)} %collective-permute-done.3, pred[]{:T(512)S(6)} %eq.4), kind=kOutput, calls=%fused_computation.53 | convolution fusion | flops 51770294272 | bytes 79691776 | tf_op jit(solution)/shard_map/dot_general | solution.py:133
  1012.5 60.4 %add_convert_fusion.6 = bf16[6144,1024]{1,0:T(8,128)(2,1)} fusion(bf16[6144,1024]{1,0:T(8,128)(2,1)} %bitcast.111, bf16[6144,4096]{1,0:T(8,128)(2,1)} %fusion.40, bf16[4096,1024]{1,0:T(8,128)(2,1)} %all-gather.17.cloned.1.call-done, bf16[4096,1024]{1,0:T(8,128)(2,1)} %collective-permute-done.4, pred[]{:T(512)S(6)} %eq.4), kind=kOutput, calls=%fused_computation.82 | convolution fusion | flops 51562676224 | bytes 92274688 | tf_op jit(solution)/shard_map/dot_general | solution.py:135
  1072.9 76.2 %fusion.48 = bf16[6144,4096]{1,0:T(8,128)(2,1)} fusion(bf16[6144,1024]{1,0:T(8,128)(2,1)} %add_convert_fusion.6, bf16[1024,4096]{1,0:T(8,128)(2,1)} %collective-permute-done.3, bf16[1024,4096]{1,0:T(8,128)(2,1)} %all-gather.15.cloned.1.call-done, pred[]{:T(512)S(6)} %eq.4), kind=kOutput, calls=%fused_computation.61 | convolution fusion | flops 51770294272 | bytes 79691776 | tf_op jit(solution)/shard_map/dot_general | solution.py:133
  1149.1 44.9 %adamw.4 = (f32[2,1,1024,4096]{3,2,1,0:T(8,128)}, f32[2,1,1024,4096]{3,2,1,0:T(8,128)}, f32[2,1,1024,4096]{3,2,1,0:T(8,128)}, bf16[1024,4096]{1,0:T(8,128)(2,1)}) custom-call(f32[1]{0:T(128)S(6)} %min.3.clip, f32[2,1,1024,4096]{3,2,1,0:T(8,128)} %w.5, f32[2,1,1024,4096]{3,2,1,0:T(8,128)} %m.5, f32[2,1,1024,4096]{3,2,1,0:T(8,128)} %v.5, ...), custom_call_target="tpu_custom_call" | custom-call | flops 83886080 | bytes 125829120 | tf_op jit(solution)/shard_map/adamw/pallas_call | solution.py:56
  1194.0 0.5 collective-permute-start.5
  1194.5 60.5 %add_convert_fusion.5 = bf16[6144,1024]{1,0:T(8,128)(2,1)} fusion(bf16[6144,1024]{1,0:T(8,128)(2,1)} %add_convert_fusion.6, bf16[6144,4096]{1,0:T(8,128)(2,1)} %fusion.48, bf16[4096,1024]{1,0:T(8,128)(2,1)} %collective-permute-done.4, bf16[4096,1024]{1,0:T(8,128)(2,1)} %all-gather.17.cloned.1.call-done, pred[]{:T(512)S(6)} %eq.4), kind=kOutput, calls=%fused_computation.81 | convolution fusion | flops 51562676224 | bytes 92274688 | tf_op jit(solution)/shard_map/dot_general | solution.py:135
  1255.0 44.9 %adamw.6 = (f32[2,1,4096,1024]{3,2,1,0:T(8,128)}, f32[2,1,4096,1024]{3,2,1,0:T(8,128)}, f32[2,1,4096,1024]{3,2,1,0:T(8,128)}, bf16[4096,1024]{1,0:T(8,128)(2,1)}) custom-call(f32[1]{0:T(128)S(6)} %min.3.clip, f32[2,1,4096,1024]{3,2,1,0:T(8,128)} %w.7, f32[2,1,4096,1024]{3,2,1,0:T(8,128)} %m.7, f32[2,1,4096,1024]{3,2,1,0:T(8,128)} %v.7, ...), custom_call_target="tpu_custom_call" | custom-call | flops 83886080 | bytes 125829120 | tf_op jit(solution)/shard_map/adamw/pallas_call | solution.py:56
  1300.0 76.4 %fusion.56 = bf16[6144,4096]{1,0:T(8,128)(2,1)} fusion(bf16[6144,1024]{1,0:T(8,128)(2,1)} %add_convert_fusion.5, bf16[1024,4096]{1,0:T(8,128)(2,1)} %get-tuple-element.99, bf16[1024,4096]{1,0:T(8,128)(2,1)} %collective-permute-done.5, pred[]{:T(512)S(6)} %eq.4), kind=kOutput, calls=%fused_computation.69 | convolution fusion | flops 51770294272 | bytes 79691776 | tf_op jit(solution)/shard_map/dot_general | solution.py:133
  1376.4 60.7 %add_convert_fusion.4 = bf16[6144,1024]{1,0:T(8,128)(2,1)} fusion(bf16[6144,1024]{1,0:T(8,128)(2,1)} %add_convert_fusion.5, bf16[6144,4096]{1,0:T(8,128)(2,1)} %fusion.56, bf16[4096,1024]{1,0:T(8,128)(2,1)} %get-tuple-element.100, bf16[4096,1024]{1,0:T(8,128)(2,1)} %collective-permute-done.6, pred[]{:T(512)S(6)} %eq.4), kind=kOutput, calls=%fused_computation.80 | convolution fusion | flops 51562676224 | bytes 92274688 | tf_op jit(solution)/shard_map/dot_general | solution.py:135
  1437.1 76.4 %fusion.64 = bf16[6144,4096]{1,0:T(8,128)(2,1)} fusion(bf16[6144,1024]{1,0:T(8,128)(2,1)} %add_convert_fusion.4, bf16[1024,4096]{1,0:T(8,128)(2,1)} %collective-permute-done.5, bf16[1024,4096]{1,0:T(8,128)(2,1)} %get-tuple-element.99, pred[]{:T(512)S(6)} %eq.4), kind=kOutput, calls=%fused_computation.77 | convolution fusion | flops 51770294272 | bytes 79691776 | tf_op jit(solution)/shard_map/dot_general | solution.py:133
  1513.5 60.6 %add_convert_fusion.3 = bf16[6144,1024]{1,0:T(8,128)(2,1)} fusion(bf16[6144,1024]{1,0:T(8,128)(2,1)} %add_convert_fusion.4, bf16[6144,4096]{1,0:T(8,128)(2,1)} %fusion.64, bf16[4096,1024]{1,0:T(8,128)(2,1)} %collective-permute-done.6, bf16[4096,1024]{1,0:T(8,128)(2,1)} %get-tuple-element.100, pred[]{:T(512)S(6)} %eq.4), kind=kOutput, calls=%fused_computation.79 | convolution fusion | flops 51562676224 | bytes 92274688 | tf_op jit(solution)/shard_map/dot_general | solution.py:135
  1574.1 0.5 collective-permute-start.7
  1574.6 44.9 %adamw.5 = (f32[2,1,1024,4096]{3,2,1,0:T(8,128)}, f32[2,1,1024,4096]{3,2,1,0:T(8,128)}, f32[2,1,1024,4096]{3,2,1,0:T(8,128)}, bf16[1024,4096]{1,0:T(8,128)(2,1)}) custom-call(f32[1]{0:T(128)S(6)} %min.3.clip, f32[2,1,1024,4096]{3,2,1,0:T(8,128)} %w.5, f32[2,1,1024,4096]{3,2,1,0:T(8,128)} %m.5, ...), custom_call_target="tpu_custom_call", output_to_operand_aliasing={{0}: (5, {}), {1}: (6, {}), {2}: (7, {})} | custom-call | flops 83886080 | bytes 125829120 | tf_op jit(solution)/shard_map/adamw/pallas_call | solution.py:56
  1619.5 44.9 %adamw.7 = (f32[2,1,4096,1024]{3,2,1,0:T(8,128)}, f32[2,1,4096,1024]{3,2,1,0:T(8,128)}, f32[2,1,4096,1024]{3,2,1,0:T(8,128)}, bf16[4096,1024]{1,0:T(8,128)(2,1)}) custom-call(f32[1]{0:T(128)S(6)} %min.3.clip, f32[2,1,4096,1024]{3,2,1,0:T(8,128)} %w.7, f32[2,1,4096,1024]{3,2,1,0:T(8,128)} %m.7, ...), custom_call_target="tpu_custom_call", output_to_operand_aliasing={{0}: (5, {}), {1}: (6, {}), {2}: (7, {})} | custom-call | flops 83886080 | bytes 125829120 | tf_op jit(solution)/shard_map/adamw/pallas_call | solution.py:56
  1664.4 24.6 %maximum_select_fusion = bf16[16,768,1024]{2,1,0:T(8,128)(2,1)} fusion(bf16[8,768,1024]{2,1,0:T(8,128)(2,1)} %collective-permute-done.7, bf16[8,768,1024]{2,1,0:T(8,128)(2,1)} %bitcast.109, pred[]{:T(512)S(6)} %eq.4), kind=kLoop, calls=%fused_computation.78 | loop fusion | flops 37748736 | bytes 50331648 | tf_op jit(solution)/shard_map/jit(_where)/select_n | solution.py:162
  (45 shorter events, 0.6 us)
Async XLA Ops:
  7.2 269.2 %reduce-scatter.7.cloned.1.call-start = ((), (), s32[]{:S(2)}) async-start(), calls=%async_computation.5 | async-start | bytes 20971520 | tf_op jit(solution)/shard_map/reduce_scatter | solution.py:106
  25.1 6.7 copy-start.2
  31.9 18.0 %copy-start = (bf16[1024,4096]{1,0:T(8,128)(2,1)}, bf16[1024,4096]{1,0:T(8,128)(2,1)S(1)}, u32[]{:S(2)}) copy-start(bf16[1024,4096]{1,0:T(8,128)(2,1)S(1)} %fusion.81) | copy-start | bytes 25165828
  31.9 18.0 %copy-start.5 = (bf16[768,1024]{1,0:T(8,128)(2,1)S(1)}, bf16[768,1024]{1,0:T(8,128)(2,1)}, u32[]{:S(2)}) copy-start(bf16[768,1024]{1,0:T(8,128)(2,1)} %param.29) | copy-start | bytes 4718596
  53.5 28.3 %collective-permute-start = (bf16[768,1024]{1,0:T(8,128)(2,1)S(1)}, bf16[768,1024]{1,0:T(8,128)(2,1)}, u32[]{:S(2)}, u32[]{:S(2)}) collective-permute-start(bf16[768,1024]{1,0:T(8,128)(2,1)S(1)} %get-tuple-element.82), channel_id=1, source_target_pairs={{1,0},{3,2},{5,4},{7,6}} | collective-permute-start | bytes 4718600 | tf_op jit(solution)/shard_map/ppermute | solution.py:100
  82.4 19.7 %copy-start.1 = (bf16[1024,4096]{1,0:T(8,128)(2,1)S(1)}, bf16[1024,4096]{1,0:T(8,128)(2,1)}, u32[]{:S(2)}) copy-start(bf16[1024,4096]{1,0:T(8,128)(2,1)} %get-tuple-element.48) | copy-start | bytes 25165828 | tf_op jit(solution)/shard_map/cond
  126.4 301.5 %reduce-scatter.11.cloned.1.call-start = ((), (), s32[]{:S(2)}) async-start(), calls=%async_computation.7 | async-start | bytes 20971520 | tf_op jit(solution)/shard_map/reduce_scatter | solution.py:104
  144.6 434.9 %reduce-scatter.5.cloned.1.call-start = ((), (), s32[]{:S(2)}) async-start(), calls=%async_computation.4 | async-start | bytes 20971520 | tf_op jit(solution)/shard_map/reduce_scatter | solution.py:106
  144.7 14.6 copy-start.3
  156.6 17.9 %slice-start = ((s8[8388608]{0:T(1024)(128)(4,1)}), s8[4194304]{0:T(1024)(128)(4,1)S(1)}, s32[]{:S(2)}) async-start(s8[8388608]{0:T(1024)(128)(4,1)} %bitcast.112), calls=%async_computation.14 | async-start | bytes 8388608
  156.6 17.9 %slice-start.1 = ((s8[8388608]{0:T(1024)(128)(4,1)}), s8[4194304]{0:T(1024)(128)(4,1)S(1)}, s32[]{:S(2)}) async-start(s8[8388608]{0:T(1024)(128)(4,1)} %bitcast.112), calls=%async_computation.15 | async-start | bytes 8388608
  156.6 17.9 %collective-permute-start.1 = (bf16[768,1024]{1,0:T(8,128)(2,1)S(1)}, bf16[768,1024]{1,0:T(8,128)(2,1)}, u32[]{:S(2)}, u32[]{:S(2)}) collective-permute-start(bf16[768,1024]{1,0:T(8,128)(2,1)S(1)} %get-tuple-element.83), channel_id=1, source_target_pairs={{0,1},{2,3},{4,5},{6,7}} | collective-permute-start | bytes 4718600 | tf_op jit(solution)/shard_map/ppermute | solution.py:107
  178.4 18.6 %collective-permute-start.2 = (bf16[768,1024]{1,0:T(8,128)(2,1)S(1)}, bf16[768,1024]{1,0:T(8,128)(2,1)}, u32[]{:S(2)}, u32[]{:S(2)}) collective-permute-start(bf16[768,1024]{1,0:T(8,128)(2,1)S(1)} %get-tuple-element.85), channel_id=1, source_target_pairs={{1,0},{3,2},{5,4},{7,6}} | collective-permute-start | bytes 4718600 | tf_op jit(solution)/shard_map/ppermute | solution.py:100
  197.0 20.1 %copy-start.4 = (bf16[2,1,768,1024]{3,2,1,0:T(8,128)(2,1)S(1)}, bf16[2,1,768,1024]{3,2,1,0:T(8,128)(2,1)}, u32[]{:S(2)}) copy-start(bf16[2,1,768,1024]{3,2,1,0:T(8,128)(2,1)} %param.28) | copy-start | bytes 9437188
  232.8 498.1 %reduce-scatter.9.cloned.1.call-start = ((), (), s32[]{:S(2)}) async-start(), calls=%async_computation.6 | async-start | bytes 20971520 | tf_op jit(solution)/shard_map/reduce_scatter | solution.py:104
  251.2 601.0 %all-gather.15.cloned.1.call-start = ((), (), s32[]{:S(2)}) async-start(), calls=%async_computation.12 | async-start | bytes 10485760 | tf_op jit(solution)/shard_map/all_gather | solution.py:119
  768.3 167.9 %all-gather.17.cloned.1.call-start = ((), (), s32[]{:S(2)}) async-start(), calls=%async_computation.13 | async-start | bytes 10485760 | tf_op jit(solution)/shard_map/all_gather | solution.py:119
  814.0 335.1 %all-gather.9.cloned.1.call-start = ((), (), s32[]{:S(2)}) async-start(), calls=%async_computation.9 | async-start | bytes 20971520 | tf_op jit(solution)/shard_map/all_gather | solution.py:119
  814.8 440.2 %all-gather.13.cloned.1.call-start = ((), (), s32[]{:S(2)}) async-start(), calls=%async_computation.11 | async-start | bytes 20971520 | tf_op jit(solution)/shard_map/all_gather | solution.py:119
  815.5 759.0 %all-gather.7.cloned.1.call-start = ((), (), s32[]{:S(2)}) async-start(), calls=%async_computation.8 | async-start | bytes 20971520 | tf_op jit(solution)/shard_map/all_gather | solution.py:119
  816.3 803.2 %all-gather.11.cloned.1.call-start = ((), (), s32[]{:S(2)}) async-start(), calls=%async_computation.10 | async-start | bytes 20971520 | tf_op jit(solution)/shard_map/all_gather | solution.py:119
  852.2 84.1 %collective-permute-start.3 = (bf16[1024,4096]{1,0:T(8,128)(2,1)}, bf16[1024,4096]{1,0:T(8,128)(2,1)}, u32[]{:S(2)}, u32[]{:S(2)}) collective-permute-start(bf16[1024,4096]{1,0:T(8,128)(2,1)} %all-gather.15.cloned.1.call-done), channel_id=1, source_target_pairs={{0,1},{1,0},{2,3},{3,2},{4,5},{5,4},{6,7},{7,6}} | collective-permute-start | bytes 25165832 | tf_op jit(solution)/shard_map/ppermute | solution.py:129
  936.3 76.2 %collective-permute-start.4 = (bf16[4096,1024]{1,0:T(8,128)(2,1)}, bf16[4096,1024]{1,0:T(8,128)(2,1)}, u32[]{:S(2)}, u32[]{:S(2)}) collective-permute-start(bf16[4096,1024]{1,0:T(8,128)(2,1)} %all-gather.17.cloned.1.call-done), channel_id=1, source_target_pairs={{0,1},{1,0},{2,3},{3,2},{4,5},{5,4},{6,7},{7,6}} | collective-permute-start | bytes 25165832 | tf_op jit(solution)/shard_map/ppermute | solution.py:129
  1194.0 105.9 %collective-permute-start.5 = (bf16[1024,4096]{1,0:T(8,128)(2,1)}, bf16[1024,4096]{1,0:T(8,128)(2,1)}, u32[]{:S(2)}, u32[]{:S(2)}) collective-permute-start(bf16[1024,4096]{1,0:T(8,128)(2,1)} %get-tuple-element.99), channel_id=1, source_target_pairs={{0,1},{1,0},{2,3},{3,2},{4,5},{5,4},{6,7},{7,6}} | collective-permute-start | bytes 25165832 | tf_op jit(solution)/shard_map/ppermute | solution.py:129
  1299.9 76.5 %collective-permute-start.6 = (bf16[4096,1024]{1,0:T(8,128)(2,1)}, bf16[4096,1024]{1,0:T(8,128)(2,1)}, u32[]{:S(2)}, u32[]{:S(2)}) collective-permute-start(bf16[4096,1024]{1,0:T(8,128)(2,1)} %get-tuple-element.100), channel_id=1, source_target_pairs={{0,1},{1,0},{2,3},{3,2},{4,5},{5,4},{6,7},{7,6}} | collective-permute-start | bytes 25165832 | tf_op jit(solution)/shard_map/ppermute | solution.py:129
  1574.1 90.3 %collective-permute-start.7 = (bf16[8,768,1024]{2,1,0:T(8,128)(2,1)}, bf16[8,768,1024]{2,1,0:T(8,128)(2,1)}, u32[]{:S(2)}, u32[]{:S(2)}) collective-permute-start(bf16[8,768,1024]{2,1,0:T(8,128)(2,1)} %bitcast.108), channel_id=1, source_target_pairs={{0,1},{1,0},{2,3},{3,2},{4,5},{5,4},{6,7},{7,6}} | collective-permute-start | bytes 37748744 | tf_op jit(solution)/shard_map/ppermute | solution.py:161
Sparse Core Ops, SparseCore 0:
  126.6 149.7 reduce-scatter.6
  279.9 147.9 reduce-scatter.10
  431.5 147.9 reduce-scatter.4
  582.9 147.9 reduce-scatter.8
  768.4 83.7 all-gather.14
  854.4 81.8 all-gather.16
  938.0 151.8 all-gather.8
  1091.7 151.8 all-gather.12
  1245.3 151.8 all-gather.6
  1398.8 151.8 all-gather.10

commit v2 on v1

--- a/solution.py
+++ b/solution.py
@@ -93,6 +93,48 @@
             back_rows = lax.dot_general(d_pre, old_up[v], CONTRACT_LAST, preferred_element_type=F32)
             return d_pre, (grad_y.astype(F32) + back_rows).astype(BF16)
 
+        y_pos, x_pos = rep // 2, rep % 2
+
+        def x_swap(t):
+            return lax.ppermute(t, 'data', [(src, src ^ 1) for src in range(replicas)])
+
+        def y_swap(t):
+            return lax.ppermute(t, 'data', [(src, src ^ 2) for src in range(replicas)])
+
+        def pick(t, idx, size):
+            return lax.dynamic_slice_in_dim(t, idx * size, size, 0)
+
+        def scatter(make, rows):
+            quarter, eighth = rows // 4, rows // 8
+            got_a = x_swap(make((1 - x_pos) * quarter, quarter))
+            got_b = y_swap(make(2 * quarter + (1 - y_pos) * quarter, quarter))
+            keep_a = make(x_pos * quarter, quarter)
+            keep_b = make(2 * quarter + y_pos * quarter, quarter)
+            send_a = pick(keep_a, 1 - y_pos, eighth) + pick(got_a, 1 - y_pos, eighth)
+            send_b = pick(keep_b, 1 - x_pos, eighth) + pick(got_b, 1 - x_pos, eighth)
+            more_a, more_b = y_swap(send_a), x_swap(send_b)
+            own_a = pick(keep_a, y_pos, eighth) + pick(got_a, y_pos, eighth)
+            own_b = pick(keep_b, x_pos, eighth) + pick(got_b, x_pos, eighth)
+            return own_a + more_a, own_b + more_b
+
+        def spread(pair):
+            a, b = pair
+            a_y, b_x = y_swap(a), x_swap(b)
+            a_x, b_y = x_swap(a), y_swap(b)
+            return [a, a_y, a_x, x_swap(a_y)], [b, b_x, b_y, y_swap(b_x)]
+
+        def join(parts):
+            parts_a, parts_b = parts
+            eighth = parts_a[0].shape[0]
+            full = jnp.zeros((8 * eighth,) + parts_a[0].shape[1:], parts_a[0].dtype)
+            for i in range(4):
+                dx, dy = i // 2, i % 2
+                at = 2 * (x_pos ^ dx) + (y_pos ^ dy)
+                full = lax.dynamic_update_slice_in_dim(full, parts_a[i], at * eighth, 0)
+                at = 4 + 2 * (y_pos ^ dx) + (x_pos ^ dy)
+                full = lax.dynamic_update_slice_in_dim(full, parts_b[i], at * eighth, 0)
+            return full
+
         def backward(v, grad_top):
             pre_act, hidden = pre_hidden(v)
             zeros = (jnp.zeros(hidden.shape, BF16), jnp.zeros(grad_top.shape, BF16))
@@ -100,30 +142,37 @@
             grad_mid = lax.ppermute(first[1], 'stage', down_hop)
             d_pre, grad_bottom = lax.cond(pos == 0, lambda g: chain(v, pre_act, g), lambda g: first, grad_mid)
             grad_y = jnp.where(pos == 1, grad_top, grad_mid)
-            sum_down = lax.dot_general(hidden, grad_y, CONTRACT_ROWS, preferred_element_type=F32) + g_down[0, v, 0]
-            part_down = lax.psum_scatter(sum_down, 'data', scatter_dimension=0, tiled=True)
-            sum_up = lax.dot_general(stash[v], d_pre, CONTRACT_ROWS, preferred_element_type=F32) + g_up[0, v, 0]
-            part_up = lax.psum_scatter(sum_up, 'data', scatter_dimension=0, tiled=True)
+            def make_down(start, size):
+                cols = lax.dynamic_slice_in_dim(hidden, start, size, 1)
+                return lax.dot_general(cols, grad_y, CONTRACT_ROWS, preferred_element_type=F32) + lax.dynamic_slice_in_dim(g_down[0, v, 0], start, size, 0)
+
+            def make_up(start, size):
+                cols = lax.dynamic_slice_in_dim(stash[v], start, size, 1)
+                return lax.dot_general(cols, d_pre, CONTRACT_ROWS, preferred_element_type=F32) + lax.dynamic_slice_in_dim(g_up[0, v, 0], start, size, 0)
+
+            part_down = scatter(make_down, hidden.shape[1])
+            part_up = scatter(make_up, stash[v].shape[1])
             return lax.ppermute(grad_bottom, 'stage', up_hop), part_up, part_down
 
         grad_flow, up1, down1 = backward(1, dy_last)
         grad_flow, up0, down0 = backward(0, grad_flow)
-        up = [up0 / replicas, up1 / replicas]
-        down = [down0 / replicas, down1 / replicas]
-
-        part_sq = sum(jnp.sum(t * t) for t in up + down)
+        up = [[t / replicas for t in pair] for pair in (up0, up1)]
+        down = [[t / replicas for t in pair] for pair in (down0, down1)]
+
+        part_sq = sum(jnp.sum(t * t) for pair in up + down for t in pair)
         total_sq = lax.psum(part_sq, ('data', 'stage'))
         clip = jnp.minimum(1.0, max_norm / (jnp.sqrt(total_sq) + 1e-6))
 
-        def gather(t):
-            return lax.all_gather(t, 'data', axis=0, tiled=True)
-
-        def shard(t, like):
-            rows = like.shape[0]
-            return lax.dynamic_slice_in_dim(t[0, 0], rep * rows, rows, 0)
-
-        def fresh_shard(w, m, v, grad):
-            return adamw_update(shard(w, grad), shard(m, grad), shard(v, grad), clip[0] * grad)[0].astype(BF16)
+        def gather(pair):
+            return join(spread(pair))
+
+        def fresh_shard(w, m, v, pair):
+            eighth = pair[0].shape[0]
+            made = []
+            for at, grad in zip((2 * x_pos + y_pos, 4 + 2 * y_pos + x_pos), pair):
+                rows = [pick(t[0, 0], at, eighth) for t in (w, m, v)]
+                made.append(adamw_update(*rows, clip[0] * grad)[0].astype(BF16))
+            return made
 
         def both(t):
             other = lax.ppermute(t, 'stage', swap)

time: 1700 us -> 2320 us (1.36)
  waiting for transfers between devices: 595 us -> 870 us
  local copies, waits for them, and re-layouts: 114 us -> 269 us
  other arithmetic: 62.6 us -> 130 us
  starting transfers between devices: 7.32 us -> 72.5 us
  matrix products: 696 us -> 730 us
  blocking collectives: 22.2 us -> 50.4 us
    ppermute x0 -> x52, waiting for transfers between devices: none -> 865 us  [the longest x26 456 us: x_swap(): return lax.ppermute(t, 'data', [(src, src ^ 1) for src in range(replicas)])]
    reduce_scatter x4 -> x0, waiting for transfers between devices: 439 us -> none  [the longest x2 292 us: backward(): lax.psum_scatter(sum_down, 'data', scatter_dimension=0, tiled=True)]
    all_gather x6 -> x0, waiting for transfers between devices: 109 us -> none  [gather(): return lax.all_gather(t, 'data', axis=0, tiled=True)]
    dynamic_update_slice x0 -> x34, local copies, waits for them, and re-layouts: none -> 68.8 us  [the longest x18 37.2 us: join(): full = lax.dynamic_update_slice_in_dim(full, parts_a[i], at * eighth, 0)]
    ppermute x0 -> x52, starting transfers between devices: none -> 62.9 us  [the longest x26 31.7 us: y_swap(): return lax.ppermute(t, 'data', [(src, src ^ 2) for src in range(replicas)])]
    dynamic_update_slice x0 -> x12, other arithmetic: none -> 53.4 us  [the longest x6 27.8 us: join(): full = lax.dynamic_update_slice_in_dim(full, parts_a[i], at * eighth, 0)]
    slice x4 -> x7, local copies, waits for them, and re-layouts: 47.4 us -> 92.6 us  [the longest x4 45.9 us: fresh_shard(): rows = [pick(t[0, 0], at, eighth) for t in (w, m, v)]]
    ppermute x2, waiting for transfers between devices: 44.3 us -> 5.06 us  [backward(): grad_mid = lax.ppermute(first[1], 'stage', down_hop)]
  transfers between devices with their start and end apart: 18 -> 60, of which waited for: 8 -> 24; matrix products, arithmetic and copies ran while one was open for 44% -> 36% of each run, Pallas kernels for 11% -> 8%
where the time goes in v2:
time: 2320 us; the launch traced here: 2310 us
  waiting for transfers between devices  870 us (38%)
  matrix products  730 us (31%)
  local copies, waits for them, and re-layouts  269 us (12%)
  Pallas kernels  180 us (8%)
  other arithmetic  130 us (6%)
  starting transfers between devices  72.5 us (3%)
  blocking collectives  50.4 us (2%)
    ppermute x26, waiting for transfers between devices, x_swap(): return lax.ppermute(t, 'data', [(src, src ^ 1) for src in range(replicas)])  456 us
    ppermute x26, waiting for transfers between devices, y_swap(): return lax.ppermute(t, 'data', [(src, src ^ 2) for src in range(replicas)])  408 us
    dot_general x4, matrix products, forward(): pre_act = jnp.dot(act, w_in, preferred_element_type=F32)  306 us
    dot_general x4, matrix products, forward(): branch = jnp.dot(hidden, w_out, preferred_element_type=F32)  242 us
    pallas_call x4, Pallas kernels, adamw_call(): pl.pallas_call(adamw_body, grid=(rows // block,), in_specs=in_specs, out_...  180 us
    dot_general x8, matrix products, make_up(): lax.dot_general(cols, d_pre, CONTRACT_ROWS, preferred_element_type=F32)  60.2 us
    psum x1, blocking collectives, sharded(): total_sq = lax.psum(part_sq, ('data', 'stage'))  50.4 us
  transfers between devices with their start and end apart: 60, of which 24 were waited for; matrix products, arithmetic and copies ran while one was open for 36% of the time, Pallas kernels for 8%

profile of v2, /device:TPU:0, one launch (start us, length us, event | category | flops | bytes accessed | tf_op | source)
XLA Modules:
  0.0 2311.1 jit_solution(10425893073143956987)
XLA Ops:
  0.6 6.5 fusion.81
  7.2 21.0 convert_bitcast_fusion
  28.1 16.0 fusion.80
  57.5 11.7 slice.68
  69.2 11.8 slice.33
  81.7 11.7 slice.73
  93.4 13.7 slice.75
  107.2 14.4 slice.74
  131.6 21.4 fusion.194
  153.0 21.9 fusion.193
  174.9 16.4 fusion.72
  191.3 28.4 %conditional.5 = ((bf16[768,4096]{1,0:T(8,128)(2,1)}, bf16[768,1024]{1,0:T(8,128)(2,1)})) conditional(s32[]{:T(128)} %convert_element_type.121, (bf16[768,4096]{1,0:T(8,128)(2,1)}, bf16[768,1024]{1,0:T(8,128)(2,1)}) %tuple.83, (bf16[768,1024]{1,0:T(8,128)(2,1)S(1)}, bf16[4096,1024]{1,0:T(8,128)(2,1)}, f32[768,4096]{1,0:T(8,128)}, ...), branch_computations={%region_2.3_spmd, %region_3.4_spmd} | conditional | flops 12950175744 | bytes 80216120 | solution.py:143
  191.5 18.4 fusion.13
  209.9 9.7 add_convert_fusion.1
  222.4 8.1 convolution_add_fusion
  230.5 8.0 convolution_add_fusion.2
  262.3 6.6 bitcast_add_fusion.3
  268.9 7.9 convolution_add_fusion.1
  276.7 7.9 convolution_add_fusion.3
  289.7 20.1 conditional.7
  289.8 19.9 fusion.32
  309.8 8.0 convolution_add_fusion.6
  320.8 6.6 bitcast_add_fusion.5
  357.7 8.6 convolution_add_fusion.7
  366.3 6.8 convolution_add_fusion.4
  373.1 50.0 %collective-permute-done.15 = f32[1024,1024]{1,0:T(8,128)} collective-permute-done((f32[1024,1024]{1,0:T(8,128)}, f32[1024,1024]{1,0:T(8,128)}, u32[]{:S(2)}, u32[]{:S(2)}) %collective-permute-start.15) | collective-permute-done | bytes 4194336 | tf_op jit(solution)/shard_map/ppermute | solution.py:99
  433.3 36.7 %collective-permute-done.8 = f32[128,4096]{1,0:T(8,128)} collective-permute-done((f32[128,4096]{1,0:T(8,128)}, f32[128,4096]{1,0:T(8,128)}, u32[]{:S(2)}, u32[]{:S(2)}) %collective-permute-start.8) | collective-permute-done | bytes 2097184 | tf_op jit(solution)/shard_map/ppermute | solution.py:102
  471.6 86.3 %collective-permute-done.10 = f32[128,4096]{1,0:T(8,128)} collective-permute-done((f32[128,4096]{1,0:T(8,128)}, f32[128,4096]{1,0:T(8,128)}, u32[]{:S(2)}, u32[]{:S(2)}) %collective-permute-start.10) | collective-permute-done | bytes 2097184 | tf_op jit(solution)/shard_map/ppermute | solution.py:99
  580.9 111.1 %collective-permute-done.16 = f32[512,1024]{1,0:T(8,128)} collective-permute-done((f32[512,1024]{1,0:T(8,128)}, f32[512,1024]{1,0:T(8,128)}, u32[]{:S(2)}, u32[]{:S(2)}) %collective-permute-start.16) | collective-permute-done | bytes 2097184 | tf_op jit(solution)/shard_map/ppermute | solution.py:102
  696.2 8.3 broadcast.201.clone.1
  730.0 10.5 collective-permute-done.4
  744.5 8.4 broadcast.200.clone
  755.4 70.7 %collective-permute-done.12 = f32[512,1024]{1,0:T(8,128)} collective-permute-done((f32[512,1024]{1,0:T(8,128)S(1)}, f32[512,1024]{1,0:T(8,128)}, u32[]{:S(2)}, u32[]{:S(2)}) %collective-permute-start.12) | collective-permute-done | bytes 2097184 | tf_op jit(solution)/shard_map/ppermute | solution.py:102
  839.5 8.0 broadcast.201.clone
  849.9 52.3 %collective-permute-done.14 = f32[512,1024]{1,0:T(8,128)S(1)} collective-permute-done((f32[512,1024]{1,0:T(8,128)S(1)}, f32[512,1024]{1,0:T(8,128)S(1)}, u32[]{:S(2)}, u32[]{:S(2)}) %collective-permute-start.14) | collective-permute-done | bytes 2097184 | tf_op jit(solution)/shard_map/ppermute | solution.py:99
  915.4 50.4 %psum.7 = f32[]{:T(128)} all-reduce(f32[]{:T(128)S(6)} %add.668), channel_id=1, replica_groups=mesh['data'=4,'stage'=2] {'data','stage'}, use_global_device_ids=true, to_apply=%region_16.17 | all-reduce | flops 1 | bytes 8 | tf_op jit(solution)/shard_map/psum | solution.py:163
  999.7 15.6 collective-permute-done.38
  1017.5 6.2 constant_dynamic-update-slice_fusion.27
  1023.7 13.2 collective-permute-done.43
  1039.4 20.9 collective-permute-done.29
  1062.2 87.9 %collective-permute-done.44 = bf16[128,4096]{1,0:T(8,128)(2,1)S(1)} collective-permute-done((bf16[128,4096]{1,0:T(8,128)(2,1)}, bf16[128,4096]{1,0:T(8,128)(2,1)S(1)}, u32[]{:S(2)}, u32[]{:S(2)}) %collective-permute-start.44) | collective-permute-done | bytes 1048608 | tf_op jit(solution)/shard_map/ppermute | solution.py:99
  1158.1 14.4 collective-permute-done.51
  1174.8 18.2 collective-permute-done.47
  1203.0 21.2 collective-permute-done.50
  1236.4 32.7 %collective-permute-done.42 = f32[512,1024]{1,0:T(8,128)} collective-permute-done((f32[512,1024]{1,0:T(8,128)}, f32[512,1024]{1,0:T(8,128)}, u32[]{:S(2)}, u32[]{:S(2)}) %collective-permute-start.42) | collective-permute-done | bytes 2097184 | tf_op jit(solution)/shard_map/ppermute | solution.py:102
  1272.6 37.7 %collective-permute-done.22 = f32[128,4096]{1,0:T(8,128)} collective-permute-done((f32[128,4096]{1,0:T(8,128)}, f32[128,4096]{1,0:T(8,128)}, u32[]{:S(2)}, u32[]{:S(2)}) %collective-permute-start.22) | collective-permute-done | bytes 2097184 | tf_op jit(solution)/shard_map/ppermute | solution.py:102
  1330.1 23.8 %collective-permute-done.32 = f32[512,1024]{1,0:T(8,128)S(1)} collective-permute-done((f32[512,1024]{1,0:T(8,128)S(1)}, f32[512,1024]{1,0:T(8,128)S(1)}, u32[]{:S(2)}, u32[]{:S(2)}) %collective-permute-start.32) | collective-permute-done | bytes 2097184 | tf_op jit(solution)/shard_map/ppermute | solution.py:99
  1366.5 32.3 %collective-permute-done.33 = f32[512,1024]{1,0:T(8,128)S(1)} collective-permute-done((f32[512,1024]{1,0:T(8,128)S(1)}, f32[512,1024]{1,0:T(8,128)S(1)}, u32[]{:S(2)}, u32[]{:S(2)}) %collective-permute-start.33) | collective-permute-done | bytes 2097184 | tf_op jit(solution)/shard_map/ppermute | solution.py:99
  1408.9 54.5 %collective-permute-done.54 = bf16[512,1024]{1,0:T(8,128)(2,1)S(1)} collective-permute-done((bf16[512,1024]{1,0:T(8,128)(2,1)}, bf16[512,1024]{1,0:T(8,128)(2,1)S(1)}, u32[]{:S(2)}, u32[]{:S(2)}) %collective-permute-start.54) | collective-permute-done | bytes 1048608 | tf_op jit(solution)/shard_map/ppermute | solution.py:99
  1479.6 32.9 %collective-permute-done.36 = f32[512,1024]{1,0:T(8,128)S(1)} collective-permute-done((f32[512,1024]{1,0:T(8,128)S(1)}, f32[512,1024]{1,0:T(8,128)S(1)}, u32[]{:S(2)}, u32[]{:S(2)}) %collective-permute-start.36) | collective-permute-done | bytes 2097184 | tf_op jit(solution)/shard_map/ppermute | solution.py:102
  1516.6 44.9 %adamw.6 = (f32[2,1,4096,1024]{3,2,1,0:T(8,128)}, f32[2,1,4096,1024]{3,2,1,0:T(8,128)}, f32[2,1,4096,1024]{3,2,1,0:T(8,128)}, bf16[4096,1024]{1,0:T(8,128)(2,1)}) custom-call(f32[1]{0:T(128)S(6)} %min.3.clip, f32[2,1,4096,1024]{3,2,1,0:T(8,128)} %w.7, f32[2,1,4096,1024]{3,2,1,0:T(8,128)} %m.7, f32[2,1,4096,1024]{3,2,1,0:T(8,128)} %v.7, ...), custom_call_target="tpu_custom_call" | custom-call | flops 83886080 | bytes 125829120 | tf_op jit(solution)/shard_map/adamw/pallas_call | solution.py:56
  1563.5 36.7 %collective-permute-done.24 = f32[128,4096]{1,0:T(8,128)S(1)} collective-permute-done((f32[128,4096]{1,0:T(8,128)S(1)}, f32[128,4096]{1,0:T(8,128)S(1)}, u32[]{:S(2)}, u32[]{:S(2)}) %collective-permute-start.24) | collective-permute-done | bytes 2097184 | tf_op jit(solution)/shard_map/ppermute | solution.py:102
  1602.6 44.9 %adamw.4 = (f32[2,1,1024,4096]{3,2,1,0:T(8,128)}, f32[2,1,1024,4096]{3,2,1,0:T(8,128)}, f32[2,1,1024,4096]{3,2,1,0:T(8,128)}, bf16[1024,4096]{1,0:T(8,128)(2,1)}) custom-call(f32[1]{0:T(128)S(6)} %min.3.clip, f32[2,1,1024,4096]{3,2,1,0:T(8,128)} %w.5, f32[2,1,1024,4096]{3,2,1,0:T(8,128)} %m.5, f32[2,1,1024,4096]{3,2,1,0:T(8,128)} %v.5, ...), custom_call_target="tpu_custom_call" | custom-call | flops 83886080 | bytes 125829120 | tf_op jit(solution)/shard_map/adamw/pallas_call | solution.py:56
  1647.5 76.6 %fusion.40 = bf16[6144,4096]{1,0:T(8,128)(2,1)} fusion(bf16[6144,1024]{1,0:T(8,128)(2,1)} %bitcast.230, bf16[1024,4096]{1,0:T(8,128)(2,1)} %constant_dynamic-update-slice_fusion.30, bf16[1024,4096]{1,0:T(8,128)(2,1)} %collective-permute-done.49, pred[]{:T(512)S(6)} %eq.6), kind=kOutput, calls=%fused_computation.53 | convolution fusion | flops 51770294272 | bytes 79691776 | tf_op jit(solution)/shard_map/dot_general | solution.py:182
  1724.2 60.5 %add_convert_fusion.6 = bf16[6144,1024]{1,0:T(8,128)(2,1)} fusion(bf16[6144,1024]{1,0:T(8,128)(2,1)} %bitcast.231, bf16[6144,4096]{1,0:T(8,128)(2,1)} %fusion.40, bf16[4096,1024]{1,0:T(8,128)(2,1)} %constant_dynamic-update-slice_fusion.23, bf16[4096,1024]{1,0:T(8,128)(2,1)} %collective-permute-done.56, pred[]{:T(512)S(6)} %eq.6), kind=kOutput, calls=%fused_computation.82 | convolution fusion | flops 51562676224 | bytes 92274688 | tf_op jit(solution)/shard_map/dot_general | solution.py:184
  1784.6 76.4 %fusion.48 = bf16[6144,4096]{1,0:T(8,128)(2,1)} fusion(bf16[6144,1024]{1,0:T(8,128)(2,1)} %add_convert_fusion.6, bf16[1024,4096]{1,0:T(8,128)(2,1)} %collective-permute-done.49, bf16[1024,4096]{1,0:T(8,128)(2,1)} %constant_dynamic-update-slice_fusion.30, pred[]{:T(512)S(6)} %eq.6), kind=kOutput, calls=%fused_computation.61 | convolution fusion | flops 51770294272 | bytes 79691776 | tf_op jit(solution)/shard_map/dot_general | solution.py:182
  1861.0 60.6 %add_convert_fusion.5 = bf16[6144,1024]{1,0:T(8,128)(2,1)} fusion(bf16[6144,1024]{1,0:T(8,128)(2,1)} %add_convert_fusion.6, bf16[6144,4096]{1,0:T(8,128)(2,1)} %fusion.48, bf16[4096,1024]{1,0:T(8,128)(2,1)} %collective-permute-done.56, bf16[4096,1024]{1,0:T(8,128)(2,1)} %constant_dynamic-update-slice_fusion.23, pred[]{:T(512)S(6)} %eq.6), kind=kOutput, calls=%fused_computation.81 | convolution fusion | flops 51562676224 | bytes 92274688 | tf_op jit(solution)/shard_map/dot_general | solution.py:184
  1921.7 76.5 %fusion.56 = bf16[6144,4096]{1,0:T(8,128)(2,1)} fusion(bf16[6144,1024]{1,0:T(8,128)(2,1)} %add_convert_fusion.5, bf16[1024,4096]{1,0:T(8,128)(2,1)} %get-tuple-element.99, bf16[1024,4096]{1,0:T(8,128)(2,1)} %collective-permute-done.57, pred[]{:T(512)S(6)} %eq.6), kind=kOutput, calls=%fused_computation.69 | convolution fusion | flops 51770294272 | bytes 79691776 | tf_op jit(solution)/shard_map/dot_general | solution.py:182
  1998.2 60.9 %add_convert_fusion.4 = bf16[6144,1024]{1,0:T(8,128)(2,1)} fusion(bf16[6144,1024]{1,0:T(8,128)(2,1)} %add_convert_fusion.5, bf16[6144,4096]{1,0:T(8,128)(2,1)} %fusion.56, bf16[4096,1024]{1,0:T(8,128)(2,1)} %get-tuple-element.100, bf16[4096,1024]{1,0:T(8,128)(2,1)} %collective-permute-done.58, pred[]{:T(512)S(6)} %eq.6), kind=kOutput, calls=%fused_computation.80 | convolution fusion | flops 51562676224 | bytes 92274688 | tf_op jit(solution)/shard_map/dot_general | solution.py:184
  2059.1 76.4 %fusion.64 = bf16[6144,4096]{1,0:T(8,128)(2,1)} fusion(bf16[6144,1024]{1,0:T(8,128)(2,1)} %add_convert_fusion.4, bf16[1024,4096]{1,0:T(8,128)(2,1)} %collective-permute-done.57, bf16[1024,4096]{1,0:T(8,128)(2,1)} %get-tuple-element.99, pred[]{:T(512)S(6)} %eq.6), kind=kOutput, calls=%fused_computation.77 | convolution fusion | flops 51770294272 | bytes 79691776 | tf_op jit(solution)/shard_map/dot_general | solution.py:182
  2135.5 60.5 %add_convert_fusion.3 = bf16[6144,1024]{1,0:T(8,128)(2,1)} fusion(bf16[6144,1024]{1,0:T(8,128)(2,1)} %add_convert_fusion.4, bf16[6144,4096]{1,0:T(8,128)(2,1)} %fusion.64, bf16[4096,1024]{1,0:T(8,128)(2,1)} %collective-permute-done.58, bf16[4096,1024]{1,0:T(8,128)(2,1)} %get-tuple-element.100, pred[]{:T(512)S(6)} %eq.6), kind=kOutput, calls=%fused_computation.79 | convolution fusion | flops 51562676224 | bytes 92274688 | tf_op jit(solution)/shard_map/dot_general | solution.py:184
  2196.4 44.9 %adamw.7 = (f32[2,1,4096,1024]{3,2,1,0:T(8,128)}, f32[2,1,4096,1024]{3,2,1,0:T(8,128)}, f32[2,1,4096,1024]{3,2,1,0:T(8,128)}, bf16[4096,1024]{1,0:T(8,128)(2,1)}) custom-call(f32[1]{0:T(128)S(6)} %min.3.clip, f32[2,1,4096,1024]{3,2,1,0:T(8,128)} %w.7, f32[2,1,4096,1024]{3,2,1,0:T(8,128)} %m.7, ...), custom_call_target="tpu_custom_call", output_to_operand_aliasing={{0}: (5, {}), {1}: (6, {}), {2}: (7, {})} | custom-call | flops 83886080 | bytes 125829120 | tf_op jit(solution)/shard_map/adamw/pallas_call | solution.py:56
  2241.3 44.9 %adamw.5 = (f32[2,1,1024,4096]{3,2,1,0:T(8,128)}, f32[2,1,1024,4096]{3,2,1,0:T(8,128)}, f32[2,1,1024,4096]{3,2,1,0:T(8,128)}, bf16[1024,4096]{1,0:T(8,128)(2,1)}) custom-call(f32[1]{0:T(128)S(6)} %min.3.clip, f32[2,1,1024,4096]{3,2,1,0:T(8,128)} %w.5, f32[2,1,1024,4096]{3,2,1,0:T(8,128)} %m.5, ...), custom_call_target="tpu_custom_call", output_to_operand_aliasing={{0}: (5, {}), {1}: (6, {}), {2}: (7, {})} | custom-call | flops 83886080 | bytes 125829120 | tf_op jit(solution)/shard_map/adamw/pallas_call | solution.py:56
  2286.2 24.6 %maximum_select_fusion = bf16[16,768,1024]{2,1,0:T(8,128)(2,1)} fusion(bf16[8,768,1024]{2,1,0:T(8,128)(2,1)} %collective-permute-done.59, bf16[8,768,1024]{2,1,0:T(8,128)(2,1)} %bitcast.233, pred[]{:T(512)S(6)} %eq.6), kind=kLoop, calls=%fused_computation.78 | loop fusion | flops 37748736 | bytes 50331648 | tf_op jit(solution)/shard_map/jit(_where)/select_n | solution.py:211
  (318 shorter events, 334.3 us)
Async XLA Ops:
  49.3 141.9 %collective-permute-start = (bf16[768,1024]{1,0:T(8,128)(2,1)}, bf16[768,1024]{1,0:T(8,128)(2,1)S(1)}, u32[]{:S(2)}, u32[]{:S(2)}) collective-permute-start(bf16[768,1024]{1,0:T(8,128)(2,1)} %copy-done.33), channel_id=1, source_target_pairs={{1,0},{3,2},{5,4},{7,6}} | collective-permute-start | bytes 4718600 | tf_op jit(solution)/shard_map/ppermute | solution.py:142
  219.7 36.0 %collective-permute-start.1 = (bf16[768,1024]{1,0:T(8,128)(2,1)}, bf16[768,1024]{1,0:T(8,128)(2,1)}, u32[]{:S(2)}, u32[]{:S(2)}) collective-permute-start(bf16[768,1024]{1,0:T(8,128)(2,1)} %get-tuple-element.83), channel_id=1, source_target_pairs={{0,1},{2,3},{4,5},{6,7}} | collective-permute-start | bytes 4718600 | tf_op jit(solution)/shard_map/ppermute | solution.py:155
  238.5 99.8 %collective-permute-start.7 = (f32[256,4096]{1,0:T(8,128)}, f32[256,4096]{1,0:T(8,128)}, u32[]{:S(2)}, u32[]{:S(2)}) collective-permute-start(f32[256,4096]{1,0:T(8,128)} %convolution_add_fusion.2), channel_id=1, source_target_pairs={{0,2},{2,0},{4,6},{6,4},{1,3},{3,1},{5,7},{7,5}} | collective-permute-start | bytes 12582920 | tf_op jit(solution)/shard_map/ppermute | solution.py:99
  241.8 101.3 %collective-permute-start.9 = (f32[256,4096]{1,0:T(8,128)}, f32[256,4096]{1,0:T(8,128)}, u32[]{:S(2)}, u32[]{:S(2)}) collective-permute-start(f32[256,4096]{1,0:T(8,128)} %convolution_add_fusion), channel_id=1, source_target_pairs={{0,4},{2,6},{4,0},{6,2},{1,5},{3,7},{5,1},{7,3}} | collective-permute-start | bytes 12582920 | tf_op jit(solution)/shard_map/ppermute | solution.py:102
  247.4 175.7 %collective-permute-start.15 = (f32[1024,1024]{1,0:T(8,128)}, f32[1024,1024]{1,0:T(8,128)}, u32[]{:S(2)}, u32[]{:S(2)}) collective-permute-start(f32[1024,1024]{1,0:T(8,128)} %bitcast_add_fusion.2), channel_id=1, source_target_pairs={{0,2},{2,0},{4,6},{6,4},{1,3},{3,1},{5,7},{7,5}} | collective-permute-start | bytes 12582920 | tf_op jit(solution)/shard_map/ppermute | solution.py:99
  251.8 176.7 %collective-permute-start.17 = (f32[1024,1024]{1,0:T(8,128)}, f32[1024,1024]{1,0:T(8,128)}, u32[]{:S(2)}, u32[]{:S(2)}) collective-permute-start(f32[1024,1024]{1,0:T(8,128)} %bitcast_add_fusion), channel_id=1, source_target_pairs={{0,4},{2,6},{4,0},{6,2},{1,5},{3,7},{5,1},{7,3}} | collective-permute-start | bytes 12582920 | tf_op jit(solution)/shard_map/ppermute | solution.py:102
  261.0 28.7 %collective-permute-start.2 = (bf16[768,1024]{1,0:T(8,128)(2,1)}, bf16[768,1024]{1,0:T(8,128)(2,1)}, u32[]{:S(2)}, u32[]{:S(2)}) collective-permute-start(bf16[768,1024]{1,0:T(8,128)(2,1)} %get-tuple-element.85), channel_id=1, source_target_pairs={{1,0},{3,2},{5,4},{7,6}} | collective-permute-start | bytes 4718600 | tf_op jit(solution)/shard_map/ppermute | solution.py:142
  317.8 252.0 %collective-permute-start.3 = (f32[256,4096]{1,0:T(8,128)}, f32[256,4096]{1,0:T(8,128)}, u32[]{:S(2)}, u32[]{:S(2)}) collective-permute-start(f32[256,4096]{1,0:T(8,128)} %convolution_add_fusion.6), channel_id=1, source_target_pairs={{0,2},{2,0},{4,6},{6,4},{1,3},{3,1},{5,7},{7,5}} | collective-permute-start | bytes 12582920 | tf_op jit(solution)/shard_map/ppermute | solution.py:99
  341.6 128.5 %collective-permute-start.8 = (f32[128,4096]{1,0:T(8,128)}, f32[128,4096]{1,0:T(8,128)}, u32[]{:S(2)}, u32[]{:S(2)}) collective-permute-start(f32[128,4096]{1,0:T(8,128)} %dynamic-slice_add_fusion.5), channel_id=1, source_target_pairs={{0,4},{2,6},{4,0},{6,2},{1,5},{3,7},{5,1},{7,3}} | collective-permute-start | bytes 6291464 | tf_op jit(solution)/shard_map/ppermute | solution.py:102
  346.3 211.7 %collective-permute-start.10 = (f32[128,4096]{1,0:T(8,128)}, f32[128,4096]{1,0:T(8,128)}, u32[]{:S(2)}, u32[]{:S(2)}) collective-permute-start(f32[128,4096]{1,0:T(8,128)} %dynamic-slice_add_fusion.4), channel_id=1, source_target_pairs={{0,2},{2,0},{4,6},{6,4},{1,3},{3,1},{5,7},{7,5}} | collective-permute-start | bytes 6291464 | tf_op jit(solution)/shard_map/ppermute | solution.py:99
  357.7 365.1 %copy-start.7 = (f32[256,4096]{1,0:T(8,128)}, f32[256,4096]{1,0:T(8,128)S(1)}, u32[]{:S(2)}) copy-start(f32[256,4096]{1,0:T(8,128)S(1)} %convolution_add_fusion.5) | copy-start | bytes 12582916
  423.1 295.3 %collective-permute-start.11 = (f32[1024,1024]{1,0:T(8,128)}, f32[1024,1024]{1,0:T(8,128)}, u32[]{:S(2)}, u32[]{:S(2)}) collective-permute-start(f32[1024,1024]{1,0:T(8,128)} %bitcast_add_fusion.6), channel_id=1, source_target_pairs={{0,2},{2,0},{4,6},{6,4},{1,3},{3,1},{5,7},{7,5}} | collective-permute-start | bytes 12582920 | tf_op jit(solution)/shard_map/ppermute | solution.py:99
  428.5 294.3 %collective-permute-start.5 = (f32[256,4096]{1,0:T(8,128)}, f32[256,4096]{1,0:T(8,128)}, u32[]{:S(2)}, u32[]{:S(2)}) collective-permute-start(f32[256,4096]{1,0:T(8,128)} %convolution_add_fusion.4), channel_id=1, source_target_pairs={{0,4},{2,6},{4,0},{6,2},{1,5},{3,7},{5,1},{7,3}} | collective-permute-start | bytes 12582920 | tf_op jit(solution)/shard_map/ppermute | solution.py:102
  470.1 256.4 %collective-permute-start.13 = (f32[1024,1024]{1,0:T(8,128)}, f32[1024,1024]{1,0:T(8,128)}, u32[]{:S(2)}, u32[]{:S(2)}) collective-permute-start(f32[1024,1024]{1,0:T(8,128)} %bitcast_add_fusion.4), channel_id=1, source_target_pairs={{0,4},{2,6},{4,0},{6,2},{1,5},{3,7},{5,1},{7,3}} | collective-permute-start | bytes 12582920 | tf_op jit(solution)/shard_map/ppermute | solution.py:102
  557.9 134.0 %collective-permute-start.16 = (f32[512,1024]{1,0:T(8,128)}, f32[512,1024]{1,0:T(8,128)}, u32[]{:S(2)}, u32[]{:S(2)}) collective-permute-start(f32[512,1024]{1,0:T(8,128)} %dynamic-slice_add_fusion.1), channel_id=1, source_target_pairs={{0,4},{2,6},{4,0},{6,2},{1,5},{3,7},{5,1},{7,3}} | collective-permute-start | bytes 6291464 | tf_op jit(solution)/shard_map/ppermute | solution.py:102
  569.8 143.8 %collective-permute-start.18 = (f32[512,1024]{1,0:T(8,128)}, f32[512,1024]{1,0:T(8,128)}, u32[]{:S(2)}, u32[]{:S(2)}) collective-permute-start(f32[512,1024]{1,0:T(8,128)} %dynamic-slice_add_fusion), channel_id=1, source_target_pairs={{0,2},{2,0},{4,6},{6,4},{1,3},{3,1},{5,7},{7,5}} | collective-permute-start | bytes 6291464 | tf_op jit(solution)/shard_map/ppermute | solution.py:99
  692.0 48.5 %collective-permute-start.4 = (f32[128,4096]{1,0:T(8,128)}, f32[128,4096]{1,0:T(8,128)}, u32[]{:S(2)}, u32[]{:S(2)}) collective-permute-start(f32[128,4096]{1,0:T(8,128)} %dynamic-slice_add_fusion.7), channel_id=1, source_target_pairs={{0,4},{2,6},{4,0},{6,2},{1,5},{3,7},{5,1},{7,3}} | collective-permute-start | bytes 6291464 | tf_op jit(solution)/shard_map/ppermute | solution.py:102
  713.7 192.9 %collective-permute-start.25 = (f32[128,4096]{1,0:T(8,128)}, f32[128,4096]{1,0:T(8,128)}, u32[]{:S(2)}, u32[]{:S(2)}) collective-permute-start(f32[128,4096]{1,0:T(8,128)} %get-tuple-element.120), channel_id=1, source_target_pairs={{0,4},{2,6},{4,0},{6,2},{1,5},{3,7},{5,1},{7,3}} | collective-permute-start | bytes 6291464 | tf_op jit(solution)/shard_map/ppermute | solution.py:102
  721.3 104.8 %collective-permute-start.12 = (f32[512,1024]{1,0:T(8,128)S(1)}, f32[512,1024]{1,0:T(8,128)}, u32[]{:S(2)}, u32[]{:S(2)}) collective-permute-start(f32[512,1024]{1,0:T(8,128)S(1)} %dynamic-slice_add_fusion.3), channel_id=1, source_target_pairs={{0,4},{2,6},{4,0},{6,2},{1,5},{3,7},{5,1},{7,3}} | collective-permute-start | bytes 6291464 | tf_op jit(solution)/shard_map/ppermute | solution.py:102
  724.7 106.0 %collective-permute-start.6 = (f32[128,4096]{1,0:T(8,128)S(1)}, f32[128,4096]{1,0:T(8,128)S(1)}, u32[]{:S(2)}, u32[]{:S(2)}) collective-permute-start(f32[128,4096]{1,0:T(8,128)S(1)} %dynamic-slice_add_fusion.6), channel_id=1, source_target_pairs={{0,2},{2,0},{4,6},{6,4},{1,3},{3,1},{5,7},{7,5}} | collective-permute-start | bytes 6291464 | tf_op jit(solution)/shard_map/ppermute | solution.py:99
  726.5 240.0 %collective-permute-start.27 = (f32[128,4096]{1,0:T(8,128)}, f32[128,4096]{1,0:T(8,128)}, u32[]{:S(2)}, u32[]{:S(2)}) collective-permute-start(f32[128,4096]{1,0:T(8,128)} %get-tuple-element.120), channel_id=1, source_target_pairs={{0,2},{2,0},{4,6},{6,4},{1,3},{3,1},{5,7},{7,5}} | collective-permute-start | bytes 6291464 | tf_op jit(solution)/shard_map/ppermute | solution.py:99
  740.5 228.3 %collective-permute-start.26 = (f32[128,4096]{1,0:T(8,128)}, f32[128,4096]{1,0:T(8,128)}, u32[]{:S(2)}, u32[]{:S(2)}) collective-permute-start(f32[128,4096]{1,0:T(8,128)} %get-tuple-element.118), channel_id=1, source_target_pairs={{0,2},{2,0},{4,6},{6,4},{1,3},{3,1},{5,7},{7,5}} | collective-permute-start | bytes 6291464 | tf_op jit(solution)/shard_map/ppermute | solution.py:99
  826.1 76.1 %collective-permute-start.14 = (f32[512,1024]{1,0:T(8,128)S(1)}, f32[512,1024]{1,0:T(8,128)S(1)}, u32[]{:S(2)}, u32[]{:S(2)}) collective-permute-start(f32[512,1024]{1,0:T(8,128)S(1)} %dynamic-slice_add_fusion.2), channel_id=1, source_target_pairs={{0,2},{2,0},{4,6},{6,4},{1,3},{3,1},{5,7},{7,5}} | collective-permute-start | bytes 6291464 | tf_op jit(solution)/shard_map/ppermute | solution.py:99
  830.7 149.2 %collective-permute-start.28 = (f32[128,4096]{1,0:T(8,128)}, f32[128,4096]{1,0:T(8,128)}, u32[]{:S(2)}, u32[]{:S(2)}) collective-permute-start(f32[128,4096]{1,0:T(8,128)} %get-tuple-element.118), channel_id=1, source_target_pairs={{0,4},{2,6},{4,0},{6,2},{1,5},{3,7},{5,1},{7,3}} | collective-permute-start | bytes 6291464 | tf_op jit(solution)/shard_map/ppermute | solution.py:102
  902.2 85.2 %collective-permute-start.37 = (f32[512,1024]{1,0:T(8,128)}, f32[512,1024]{1,0:T(8,128)}, u32[]{:S(2)}, u32[]{:S(2)}) collective-permute-start(f32[512,1024]{1,0:T(8,128)} %get-tuple-element.112), channel_id=1, source_target_pairs={{0,4},{2,6},{4,0},{6,2},{1,5},{3,7},{5,1},{7,3}} | collective-permute-start | bytes 6291464 | tf_op jit(solution)/shard_map/ppermute | solution.py:102
  906.5 81.4 %collective-permute-start.39 = (f32[512,1024]{1,0:T(8,128)}, f32[512,1024]{1,0:T(8,128)}, u32[]{:S(2)}, u32[]{:S(2)}) collective-permute-start(f32[512,1024]{1,0:T(8,128)} %get-tuple-element.112), channel_id=1, source_target_pairs={{0,2},{2,0},{4,6},{6,4},{1,3},{3,1},{5,7},{7,5}} | collective-permute-start | bytes 6291464 | tf_op jit(solution)/shard_map/ppermute | solution.py:99
  966.5 48.8 %collective-permute-start.38 = (f32[512,1024]{1,0:T(8,128)}, f32[512,1024]{1,0:T(8,128)}, u32[]{:S(2)}, u32[]{:S(2)}) collective-permute-start(f32[512,1024]{1,0:T(8,128)} %copy-done.16), channel_id=1, source_target_pairs={{0,2},{2,0},{4,6},{6,4},{1,3},{3,1},{5,7},{7,5}} | collective-permute-start | bytes 6291464 | tf_op jit(solution)/shard_map/ppermute | solution.py:99
  968.8 48.5 %collective-permute-start.40 = (f32[512,1024]{1,0:T(8,128)}, f32[512,1024]{1,0:T(8,128)S(1)}, u32[]{:S(2)}, u32[]{:S(2)}) collective-permute-start(f32[512,1024]{1,0:T(8,128)} %copy-done.16), channel_id=1, source_target_pairs={{0,4},{2,6},{4,0},{6,2},{1,5},{3,7},{5,1},{7,3}} | collective-permute-start | bytes 6291464 | tf_op jit(solution)/shard_map/ppermute | solution.py:102
  979.9 80.3 %collective-permute-start.29 = (f32[128,4096]{1,0:T(8,128)}, f32[128,4096]{1,0:T(8,128)}, u32[]{:S(2)}, u32[]{:S(2)}) collective-permute-start(f32[128,4096]{1,0:T(8,128)} %collective-permute-done.25), channel_id=1, source_target_pairs={{0,2},{2,0},{4,6},{6,4},{1,3},{3,1},{5,7},{7,5}} | collective-permute-start | bytes 6291464 | tf_op jit(solution)/shard_map/ppermute | solution.py:99
  981.4 242.8 %slice-start.22 = ((s8[25165824]{0:T(1024)(128)(4,1)}), s8[4194304]{0:T(1024)(128)(4,1)S(1)}, s32[]{:S(2)}) async-start(s8[25165824]{0:T(1024)(128)(4,1)} %bitcast.236), calls=%async_computation.22 | async-start | bytes 8388608
  981.4 242.8 %slice-start.23 = ((s8[25165824]{0:T(1024)(128)(4,1)}), s8[4194304]{0:T(1024)(128)(4,1)S(1)}, s32[]{:S(2)}) async-start(s8[25165824]{0:T(1024)(128)(4,1)} %bitcast.236), calls=%async_computation.23 | async-start | bytes 8388608
  987.4 165.8 %collective-permute-start.41 = (f32[512,1024]{1,0:T(8,128)}, f32[512,1024]{1,0:T(8,128)}, u32[]{:S(2)}, u32[]{:S(2)}) collective-permute-start(f32[512,1024]{1,0:T(8,128)} %collective-permute-done.37), channel_id=1, source_target_pairs={{0,2},{2,0},{4,6},{6,4},{1,3},{3,1},{5,7},{7,5}} | collective-permute-start | bytes 6291464 | tf_op jit(solution)/shard_map/ppermute | solution.py:99
  988.0 236.2 %slice-start.24 = ((s8[25165824]{0:T(1024)(128)(4,1)}), s8[4194304]{0:T(1024)(128)(4,1)S(1)}, s32[]{:S(2)}) async-start(s8[25165824]{0:T(1024)(128)(4,1)} %bitcast.236), calls=%async_computation.24 | async-start | bytes 8388608
  988.0 48.9 %collective-permute-start.43 = (bf16[128,4096]{1,0:T(8,128)(2,1)}, bf16[128,4096]{1,0:T(8,128)(2,1)S(1)}, u32[]{:S(2)}, u32[]{:S(2)}) collective-permute-start(bf16[128,4096]{1,0:T(8,128)(2,1)} %get-tuple-element.108), channel_id=1, source_target_pairs={{0,4},{2,6},{4,0},{6,2},{1,5},{3,7},{5,1},{7,3}} | collective-permute-start | bytes 3145736 | tf_op jit(solution)/shard_map/ppermute | solution.py:102
  1015.3 138.7 %collective-permute-start.45 = (bf16[128,4096]{1,0:T(8,128)(2,1)}, bf16[128,4096]{1,0:T(8,128)(2,1)S(1)}, u32[]{:S(2)}, u32[]{:S(2)}) collective-permute-start(bf16[128,4096]{1,0:T(8,128)(2,1)} %get-tuple-element.108), channel_id=1, source_target_pairs={{0,2},{2,0},{4,6},{6,4},{1,3},{3,1},{5,7},{7,5}} | collective-permute-start | bytes 3145736 | tf_op jit(solution)/shard_map/ppermute | solution.py:99
  1017.3 132.8 %collective-permute-start.44 = (bf16[128,4096]{1,0:T(8,128)(2,1)}, bf16[128,4096]{1,0:T(8,128)(2,1)S(1)}, u32[]{:S(2)}, u32[]{:S(2)}) collective-permute-start(bf16[128,4096]{1,0:T(8,128)(2,1)} %get-tuple-element.106), channel_id=1, source_target_pairs={{0,2},{2,0},{4,6},{6,4},{1,3},{3,1},{5,7},{7,5}} | collective-permute-start | bytes 3145736 | tf_op jit(solution)/shard_map/ppermute | solution.py:99
  1036.8 119.4 %collective-permute-start.46 = (bf16[128,4096]{1,0:T(8,128)(2,1)}, bf16[128,4096]{1,0:T(8,128)(2,1)S(1)}, u32[]{:S(2)}, u32[]{:S(2)}) collective-permute-start(bf16[128,4096]{1,0:T(8,128)(2,1)} %get-tuple-element.106), channel_id=1, source_target_pairs={{0,4},{2,6},{4,0},{6,2},{1,5},{3,7},{5,1},{7,3}} | collective-permute-start | bytes 3145736 | tf_op jit(solution)/shard_map/ppermute | solution.py:102
  1060.2 112.4 %collective-permute-start.51 = (bf16[512,1024]{1,0:T(8,128)(2,1)S(1)}, bf16[512,1024]{1,0:T(8,128)(2,1)S(1)}, u32[]{:S(2)}, u32[]{:S(2)}) collective-permute-start(bf16[512,1024]{1,0:T(8,128)(2,1)S(1)} %get-tuple-element.102), channel_id=1, source_target_pairs={{0,2},{2,0},{4,6},{6,4},{1,3},{3,1},{5,7},{7,5}} | collective-permute-start | bytes 3145736 | tf_op jit(solution)/shard_map/ppermute | solution.py:99
  1150.1 42.9 %collective-permute-start.47 = (bf16[128,4096]{1,0:T(8,128)(2,1)S(1)}, bf16[128,4096]{1,0:T(8,128)(2,1)S(1)}, u32[]{:S(2)}, u32[]{:S(2)}) collective-permute-start(bf16[128,4096]{1,0:T(8,128)(2,1)S(1)} %collective-permute-done.43), channel_id=1, source_target_pairs={{0,2},{2,0},{4,6},{6,4},{1,3},{3,1},{5,7},{7,5}} | collective-permute-start | bytes 3145736 | tf_op jit(solution)/shard_map/ppermute | solution.py:99
  1153.2 42.3 %collective-permute-start.53 = (bf16[512,1024]{1,0:T(8,128)(2,1)S(1)}, bf16[512,1024]{1,0:T(8,128)(2,1)S(1)}, u32[]{:S(2)}, u32[]{:S(2)}) collective-permute-start(bf16[512,1024]{1,0:T(8,128)(2,1)S(1)} %get-tuple-element.102), channel_id=1, source_target_pairs={{0,4},{2,6},{4,0},{6,2},{1,5},{3,7},{5,1},{7,3}} | collective-permute-start | bytes 3145736 | tf_op jit(solution)/shard_map/ppermute | solution.py:102
  1154.0 47.7 %collective-permute-start.48 = (bf16[128,4096]{1,0:T(8,128)(2,1)S(1)}, bf16[128,4096]{1,0:T(8,128)(2,1)S(1)}, u32[]{:S(2)}, u32[]{:S(2)}) collective-permute-start(bf16[128,4096]{1,0:T(8,128)(2,1)S(1)} %collective-permute-done.44), channel_id=1, source_target_pairs={{0,4},{2,6},{4,0},{6,2},{1,5},{3,7},{5,1},{7,3}} | collective-permute-start | bytes 3145736 | tf_op jit(solution)/shard_map/ppermute | solution.py:102
  1156.3 67.9 %collective-permute-start.50 = (bf16[512,1024]{1,0:T(8,128)(2,1)}, bf16[512,1024]{1,0:T(8,128)(2,1)}, u32[]{:S(2)}, u32[]{:S(2)}) collective-permute-start(bf16[512,1024]{1,0:T(8,128)(2,1)} %get-tuple-element.104), channel_id=1, source_target_pairs={{0,4},{2,6},{4,0},{6,2},{1,5},{3,7},{5,1},{7,3}} | collective-permute-start | bytes 3145736 | tf_op jit(solution)/shard_map/ppermute | solution.py:102
  1172.6 96.5 %collective-permute-start.42 = (f32[512,1024]{1,0:T(8,128)}, f32[512,1024]{1,0:T(8,128)}, u32[]{:S(2)}, u32[]{:S(2)}) collective-permute-start(f32[512,1024]{1,0:T(8,128)} %collective-permute-done.38), channel_id=1, source_target_pairs={{0,4},{2,6},{4,0},{6,2},{1,5},{3,7},{5,1},{7,3}} | collective-permute-start | bytes 6291464 | tf_op jit(solution)/shard_map/ppermute | solution.py:102
  1193.0 36.7 %collective-permute-start.52 = (bf16[512,1024]{1,0:T(8,128)(2,1)}, bf16[512,1024]{1,0:T(8,128)(2,1)}, u32[]{:S(2)}, u32[]{:S(2)}) collective-permute-start(bf16[512,1024]{1,0:T(8,128)(2,1)} %get-tuple-element.104), channel_id=1, source_target_pairs={{0,2},{2,0},{4,6},{6,4},{1,3},{3,1},{5,7},{7,5}} | collective-permute-start | bytes 3145736 | tf_op jit(solution)/shard_map/ppermute | solution.py:99
  1195.5 114.8 %collective-permute-start.22 = (f32[128,4096]{1,0:T(8,128)}, f32[128,4096]{1,0:T(8,128)}, u32[]{:S(2)}, u32[]{:S(2)}) collective-permute-start(f32[128,4096]{1,0:T(8,128)} %get-tuple-element.121), channel_id=1, source_target_pairs={{0,4},{2,6},{4,0},{6,2},{1,5},{3,7},{5,1},{7,3}} | collective-permute-start | bytes 6291464 | tf_op jit(solution)/shard_map/ppermute | solution.py:102
  1201.7 116.8 %collective-permute-start.20 = (f32[128,4096]{1,0:T(8,128)}, f32[128,4096]{1,0:T(8,128)S(1)}, u32[]{:S(2)}, u32[]{:S(2)}) collective-permute-start(f32[128,4096]{1,0:T(8,128)} %get-tuple-element.121), channel_id=1, source_target_pairs={{0,2},{2,0},{4,6},{6,4},{1,3},{3,1},{5,7},{7,5}} | collective-permute-start | bytes 6291464 | tf_op jit(solution)/shard_map/ppermute | solution.py:99
  1224.2 423.4 %collective-permute-start.49 = (bf16[1024,4096]{1,0:T(8,128)(2,1)}, bf16[1024,4096]{1,0:T(8,128)(2,1)}, u32[]{:S(2)}, u32[]{:S(2)}) collective-permute-start(bf16[1024,4096]{1,0:T(8,128)(2,1)} %constant_dynamic-update-slice_fusion.30), channel_id=1, source_target_pairs={{0,1},{1,0},{2,3},{3,2},{4,5},{5,4},{6,7},{7,6}} | collective-permute-start | bytes 25165832 | tf_op jit(solution)/shard_map/ppermute | solution.py:178
  1229.7 94.8 %collective-permute-start.21 = (f32[128,4096]{1,0:T(8,128)}, f32[128,4096]{1,0:T(8,128)S(1)}, u32[]{:S(2)}, u32[]{:S(2)}) collective-permute-start(f32[128,4096]{1,0:T(8,128)} %get-tuple-element.123), channel_id=1, source_target_pairs={{0,2},{2,0},{4,6},{6,4},{1,3},{3,1},{5,7},{7,5}} | collective-permute-start | bytes 6291464 | tf_op jit(solution)/shard_map/ppermute | solution.py:99
  1269.1 84.8 %collective-permute-start.32 = (f32[512,1024]{1,0:T(8,128)S(1)}, f32[512,1024]{1,0:T(8,128)S(1)}, u32[]{:S(2)}, u32[]{:S(2)}) collective-permute-start(f32[512,1024]{1,0:T(8,128)S(1)} %copy-done.27), channel_id=1, source_target_pairs={{0,2},{2,0},{4,6},{6,4},{1,3},{3,1},{5,7},{7,5}} | collective-permute-start | bytes 6291464 | tf_op jit(solution)/shard_map/ppermute | solution.py:99
  1310.3 48.5 %collective-permute-start.31 = (f32[512,1024]{1,0:T(8,128)S(1)}, f32[512,1024]{1,0:T(8,128)S(1)}, u32[]{:S(2)}, u32[]{:S(2)}) collective-permute-start(f32[512,1024]{1,0:T(8,128)S(1)} %copy-done.28), channel_id=1, source_target_pairs={{0,4},{2,6},{4,0},{6,2},{1,5},{3,7},{5,1},{7,3}} | collective-permute-start | bytes 6291464 | tf_op jit(solution)/shard_map/ppermute | solution.py:102
  1318.5 80.3 %collective-permute-start.33 = (f32[512,1024]{1,0:T(8,128)S(1)}, f32[512,1024]{1,0:T(8,128)S(1)}, u32[]{:S(2)}, u32[]{:S(2)}) collective-permute-start(f32[512,1024]{1,0:T(8,128)S(1)} %copy-done.28), channel_id=1, source_target_pairs={{0,2},{2,0},{4,6},{6,4},{1,3},{3,1},{5,7},{7,5}} | collective-permute-start | bytes 6291464 | tf_op jit(solution)/shard_map/ppermute | solution.py:99
  1324.6 81.4 %collective-permute-start.19 = (f32[128,4096]{1,0:T(8,128)S(1)}, f32[128,4096]{1,0:T(8,128)S(1)}, u32[]{:S(2)}, u32[]{:S(2)}) collective-permute-start(f32[128,4096]{1,0:T(8,128)S(1)} %copy-done.26), channel_id=1, source_target_pairs={{0,4},{2,6},{4,0},{6,2},{1,5},{3,7},{5,1},{7,3}} | collective-permute-start | bytes 6291464 | tf_op jit(solution)/shard_map/ppermute | solution.py:102
  1353.9 111.7 %collective-permute-start.34 = (f32[512,1024]{1,0:T(8,128)S(1)}, f32[512,1024]{1,0:T(8,128)S(1)}, u32[]{:S(2)}, u32[]{:S(2)}) collective-permute-start(f32[512,1024]{1,0:T(8,128)S(1)} %copy-done.27), channel_id=1, source_target_pairs={{0,4},{2,6},{4,0},{6,2},{1,5},{3,7},{5,1},{7,3}} | collective-permute-start | bytes 6291464 | tf_op jit(solution)/shard_map/ppermute | solution.py:102
  1358.8 111.2 %collective-permute-start.35 = (f32[512,1024]{1,0:T(8,128)S(1)}, f32[512,1024]{1,0:T(8,128)S(1)}, u32[]{:S(2)}, u32[]{:S(2)}) collective-permute-start(f32[512,1024]{1,0:T(8,128)S(1)} %collective-permute-done.31), channel_id=1, source_target_pairs={{0,2},{2,0},{4,6},{6,4},{1,3},{3,1},{5,7},{7,5}} | collective-permute-start | bytes 6291464 | tf_op jit(solution)/shard_map/ppermute | solution.py:99
  1398.8 64.5 %collective-permute-start.54 = (bf16[512,1024]{1,0:T(8,128)(2,1)}, bf16[512,1024]{1,0:T(8,128)(2,1)S(1)}, u32[]{:S(2)}, u32[]{:S(2)}) collective-permute-start(bf16[512,1024]{1,0:T(8,128)(2,1)} %collective-permute-done.50), channel_id=1, source_target_pairs={{0,2},{2,0},{4,6},{6,4},{1,3},{3,1},{5,7},{7,5}} | collective-permute-start | bytes 3145736 | tf_op jit(solution)/shard_map/ppermute | solution.py:99
  1406.0 62.9 %collective-permute-start.55 = (bf16[512,1024]{1,0:T(8,128)(2,1)S(1)}, bf16[512,1024]{1,0:T(8,128)(2,1)S(1)}, u32[]{:S(2)}, u32[]{:S(2)}) collective-permute-start(bf16[512,1024]{1,0:T(8,128)(2,1)S(1)} %collective-permute-done.51), channel_id=1, source_target_pairs={{0,4},{2,6},{4,0},{6,2},{1,5},{3,7},{5,1},{7,3}} | collective-permute-start | bytes 3145736 | tf_op jit(solution)/shard_map/ppermute | solution.py:102
  1463.4 49.1 %collective-permute-start.36 = (f32[512,1024]{1,0:T(8,128)S(1)}, f32[512,1024]{1,0:T(8,128)S(1)}, u32[]{:S(2)}, u32[]{:S(2)}) collective-permute-start(f32[512,1024]{1,0:T(8,128)S(1)} %collective-permute-done.32), channel_id=1, source_target_pairs={{0,4},{2,6},{4,0},{6,2},{1,5},{3,7},{5,1},{7,3}} | collective-permute-start | bytes 6291464 | tf_op jit(solution)/shard_map/ppermute | solution.py:102
  1465.6 95.9 %collective-permute-start.23 = (f32[128,4096]{1,0:T(8,128)S(1)}, f32[128,4096]{1,0:T(8,128)S(1)}, u32[]{:S(2)}, u32[]{:S(2)}) collective-permute-start(f32[128,4096]{1,0:T(8,128)S(1)} %collective-permute-done.19), channel_id=1, source_target_pairs={{0,2},{2,0},{4,6},{6,4},{1,3},{3,1},{5,7},{7,5}} | collective-permute-start | bytes 6291464 | tf_op jit(solution)/shard_map/ppermute | solution.py:99
  1468.9 94.6 %collective-permute-start.30 = (f32[128,4096]{1,0:T(8,128)}, f32[128,4096]{1,0:T(8,128)S(1)}, u32[]{:S(2)}, u32[]{:S(2)}) collective-permute-start(f32[128,4096]{1,0:T(8,128)} %collective-permute-done.26), channel_id=1, source_target_pairs={{0,4},{2,6},{4,0},{6,2},{1,5},{3,7},{5,1},{7,3}} | collective-permute-start | bytes 6291464 | tf_op jit(solution)/shard_map/ppermute | solution.py:102
  1470.0 130.1 %collective-permute-start.24 = (f32[128,4096]{1,0:T(8,128)S(1)}, f32[128,4096]{1,0:T(8,128)S(1)}, u32[]{:S(2)}, u32[]{:S(2)}) collective-permute-start(f32[128,4096]{1,0:T(8,128)S(1)} %collective-permute-done.20), channel_id=1, source_target_pairs={{0,4},{2,6},{4,0},{6,2},{1,5},{3,7},{5,1},{7,3}} | collective-permute-start | bytes 6291464 | tf_op jit(solution)/shard_map/ppermute | solution.py:102
  1512.5 211.7 %collective-permute-start.56 = (bf16[4096,1024]{1,0:T(8,128)(2,1)}, bf16[4096,1024]{1,0:T(8,128)(2,1)}, u32[]{:S(2)}, u32[]{:S(2)}) collective-permute-start(bf16[4096,1024]{1,0:T(8,128)(2,1)} %constant_dynamic-update-slice_fusion.23), channel_id=1, source_target_pairs={{0,1},{1,0},{2,3},{3,2},{4,5},{5,4},{6,7},{7,6}} | collective-permute-start | bytes 25165832 | tf_op jit(solution)/shard_map/ppermute | solution.py:178
  1561.5 436.7 %collective-permute-start.58 = (bf16[4096,1024]{1,0:T(8,128)(2,1)}, bf16[4096,1024]{1,0:T(8,128)(2,1)}, u32[]{:S(2)}, u32[]{:S(2)}) collective-permute-start(bf16[4096,1024]{1,0:T(8,128)(2,1)} %get-tuple-element.100), channel_id=1, source_target_pairs={{0,1},{1,0},{2,3},{3,2},{4,5},{5,4},{6,7},{7,6}} | collective-permute-start | bytes 25165832 | tf_op jit(solution)/shard_map/ppermute | solution.py:178
  1647.5 274.2 %collective-permute-start.57 = (bf16[1024,4096]{1,0:T(8,128)(2,1)}, bf16[1024,4096]{1,0:T(8,128)(2,1)}, u32[]{:S(2)}, u32[]{:S(2)}) collective-permute-start(bf16[1024,4096]{1,0:T(8,128)(2,1)} %get-tuple-element.99), channel_id=1, source_target_pairs={{0,1},{1,0},{2,3},{3,2},{4,5},{5,4},{6,7},{7,6}} | collective-permute-start | bytes 25165832 | tf_op jit(solution)/shard_map/ppermute | solution.py:178
  2196.0 90.3 %collective-permute-start.59 = (bf16[8,768,1024]{2,1,0:T(8,128)(2,1)}, bf16[8,768,1024]{2,1,0:T(8,128)(2,1)}, u32[]{:S(2)}, u32[]{:S(2)}) collective-permute-start(bf16[8,768,1024]{2,1,0:T(8,128)(2,1)} %bitcast.232), channel_id=1, source_target_pairs={{0,1},{1,0},{2,3},{3,2},{4,5},{5,4},{6,7},{7,6}} | collective-permute-start | bytes 37748744 | tf_op jit(solution)/shard_map/ppermute | solution.py:210
  (61 other events, 1855.1 us)

commit v3 on v1

v3 whole, which is shorter than its diff:
```python
import functools

import jax
import jax.numpy as jnp
from jax import lax
from jax.experimental import pallas as pl
from jax.experimental.pallas import tpu as pltpu
from jax.sharding import PartitionSpec as P

LR = 0.002
BETA1 = 0.9
BETA2 = 0.95
ADAM_EPS = 1e-8
WDECAY = 0.1
BIAS_ONE = 1.0 - BETA1 ** 10
BIAS_TWO = 1.0 - BETA2 ** 10
CONTRACT_ROWS = (((0,), (0,)), ((), ()))
CONTRACT_LAST = (((1,), (1,)), ((), ()))
F32 = jnp.float32
BF16 = jnp.bfloat16
D_MODEL, D_FF = 1024, 4096
ROW_TILE = 384
FF_TILE = 1024
CORE_TILES = 16
TILE = {'up': (64, D_FF), 'down': (256, D_MODEL)}
N_TILES = 16
OWN_TILES = 4
STRIP = 8


def gelu_tanh(pre_act):
    return jax.nn.gelu(pre_act, approximate=True)


def adamw_update(weight, mom, vel, grad):
    mom_new = BETA1 * mom + (1.0 - BETA1) * grad
    vel_new = BETA2 * vel + (1.0 - BETA2) * grad * grad
    step_dir = mom_new * (BIAS_TWO ** 0.5 / BIAS_ONE) / (jnp.sqrt(vel_new) + ADAM_EPS * BIAS_TWO ** 0.5)
    return weight - LR * (step_dir + WDECAY * weight), mom_new, vel_new


class Job:
    def __init__(self, kind, virtual, own):
        self.kind, self.virtual, self.own = kind, virtual, own
        self.count = OWN_TILES if own else N_TILES - OWN_TILES


class Plan:
    pass


def fused_kernel(plan, place, *refs):
    refs = list(refs)

    def take(count):
        return [refs.pop(0) for _ in range(count)]

    step = pl.program_id(0)
    slot = lax.rem(step, 2)
    pos, rep = place[0], place[1]
    clip, = take(1)
    if plan.rows:
        x_ref, *weights = take(5)
    state = {kind: take(3) for kind in plan.kinds}
    grads = {kind: take(1)[0] for kind in plan.kinds}
    take(plan.n_alias)
    y_refs = take(plan.n_act)
    outs = {kind: take(3) for kind in plan.kinds}
    fresh = {kind: take(1)[0] for kind in plan.kinds if plan.fresh}
    if plan.rows:
        w_in, w_out, hidden, w_sem = take(4)
    bufs = {kind: take(5 if plan.fresh else 4) for kind in plan.kinds}

    def rows_of(kind, job, t):
        size = TILE[kind][0]
        if job.own:
            src, dst = t, rep * OWN_TILES + t
        else:
            src = dst = lax.rem(rep * OWN_TILES + OWN_TILES + t, N_TILES)
        return pl.multiple_of(src * size, size), pl.multiple_of(dst * size, size), size

    def loads(kind, job, t, where):
        src, dst, size = rows_of(kind, job, t)
        ins, sem = bufs[kind][0], bufs[kind][-2]
        refs_in = [ref.at[job.virtual, 0, pl.ds(dst, size), :] for ref in state[kind]] + [grads[kind].at[pl.ds(src, size), :]]
        return [pltpu.make_async_copy(ref, ins.at[where, j], sem.at[where, j]) for j, ref in enumerate(refs_in)]

    def stores(kind, job, t, where):
        src, dst, size = rows_of(kind, job, t)
        made, sem = bufs[kind][1], bufs[kind][-1]
        copies = [pltpu.make_async_copy(made.at[where, j], ref.at[job.virtual, 0, pl.ds(dst, size), :], sem.at[where, j])
                  for j, ref in enumerate(outs[kind])]
        if plan.fresh:
            row = src if plan.fresh == 'own' else dst
            copies.append(pltpu.make_async_copy(bufs[kind][2].at[where], fresh[kind].at[pl.ds(row, size), :], sem.at[where, 3]))
        return copies

    def for_step(at, make, where, wait):
        for kind in plan.kinds:
            job = plan.jobs[kind]
            @pl.when((at >= 0) & (at < job.count))
            def _(kind=kind, job=job):
                for copy in make(kind, job, at, where):
                    copy.wait() if wait else copy.start()

    def fill(which):
        for j, dst in enumerate((w_in, w_out)):
            pltpu.make_async_copy(weights[2 * j + which], dst, w_sem.at[j]).start()

    @pl.when(step == 0)
    def _():
        for_step(step, loads, 0, False)
        if plan.rows:
            pl.when(pos == plan.owner)(lambda: fill(0))
            pl.when(pos != plan.owner)(lambda: fill(1))

    for_step(step + 1, loads, 1 - slot, False)
    for_step(step, loads, slot, True)
    for_step(step - 2, stores, slot, True)

    if plan.rows:
        @pl.when(step == 0)
        def _():
            for j, dst in enumerate((w_in, w_out)):
                pltpu.make_async_copy(weights[2 * j], dst, w_sem.at[j]).wait()

        for at in range(0, D_FF, FF_TILE):
            part = jnp.dot(x_ref[...], w_in[:, at:at + FF_TILE], preferred_element_type=F32)
            hidden[:, at:at + FF_TILE] = gelu_tanh(part).astype(BF16)
        out = jnp.dot(hidden[...], w_out[...], preferred_element_type=F32)
        out = (x_ref[...].astype(F32) + out).astype(BF16)
        for y_ref in y_refs:
            y_ref[...] = out

    scale = clip[0]
    for kind in plan.kinds:
        ins, made = bufs[kind][0], bufs[kind][1]
        for row in range(0, TILE[kind][0], STRIP):
            for col in range(0, TILE[kind][1], D_MODEL):
                at = (pl.ds(row, STRIP), pl.ds(col, D_MODEL))
                old = [ins[(slot, j) + at] for j in range(4)]
                new = adamw_update(old[0], old[1], old[2], scale * old[3])
                for j in range(3):
                    made[(slot, j) + at] = new[j]
                if plan.fresh:
                    bufs[kind][2][(slot,) + at] = new[0].astype(BF16)

    for_step(step, stores, slot, False)

    @pl.when(step == plan.steps - 1)
    def _():
        for_step(step - 1, stores, 1 - slot, True)
        for_step(step, stores, slot, True)


def fused_call(name, place, clip, jobs, state, grads, prev, fresh, act=None, weights=None, owner=0, first=False, last=False):
    plan = Plan()
    plan.kinds = tuple(kind for kind in ('up', 'down') if kind in jobs)
    plan.jobs, plan.owner, plan.rows, plan.fresh = jobs, owner, act is not None, fresh
    plan.steps = CORE_TILES if plan.rows else max(job.count for job in jobs.values())
    hbm = pl.BlockSpec(memory_space=pl.ANY)
    in_specs, args = [pl.BlockSpec(memory_space=pltpu.SMEM)], [clip]
    out_specs, out_shape, scratch = [], [], []
    tile = (ROW_TILE, D_MODEL)

    def here(i, place):
        return (i, 0)

    def among_both(i, place):
        return (place[0] * CORE_TILES + i, 0)

    if plan.rows:
        in_specs += [pl.BlockSpec(tile, among_both if first else here)] + [hbm] * 4
        args += [act, *weights]
        out_specs.append(pl.BlockSpec(tile, here))
        out_shape.append(jax.ShapeDtypeStruct((CORE_TILES * ROW_TILE, D_MODEL), BF16))
        if last:
            out_specs.append(pl.BlockSpec(tile, among_both))
            out_shape.append(jax.ShapeDtypeStruct((2 * CORE_TILES * ROW_TILE, D_MODEL), BF16))
        scratch += [pltpu.VMEM((D_MODEL, D_FF), BF16), pltpu.VMEM((D_FF, D_MODEL), BF16), pltpu.VMEM((ROW_TILE, D_FF), BF16), pltpu.SemaphoreType.DMA((2,))]
    plan.n_act = len(out_shape)
    for kind in plan.kinds:
        args += list(state[kind])
    args += [grads[kind] for kind in plan.kinds]
    aliases = {}
    for kind in plan.kinds:
        for j, arr in enumerate(prev.get(kind, (None,) * 3)[:3]):
            if arr is not None:
                aliases[1 + len(args)] = len(out_shape)
                args.append(arr)
            out_shape.append(jax.ShapeDtypeStruct(state[kind][j].shape, F32))
    if fresh:
        for kind in plan.kinds:
            arr = prev.get(kind, (None,) * 4)[3]
            if arr is not None and fresh != 'own':
                aliases[1 + len(args)] = len(out_shape)
                args.append(arr)
            rows, cols = state[kind][0].shape[2:]
            out_shape.append(jax.ShapeDtypeStruct((rows // 4 if fresh == 'own' else rows, cols), BF16))
    plan.n_alias = len(aliases)
    in_specs += [hbm] * (len(args) - len(in_specs))
    out_specs += [hbm] * (len(out_shape) - len(out_specs))
    for kind in plan.kinds:
        scratch += [pltpu.VMEM((2, 4) + TILE[kind], F32), pltpu.VMEM((2, 3) + TILE[kind], F32)]
        if fresh:
            scratch.append(pltpu.VMEM((2,) + TILE[kind], BF16))
        scratch += [pltpu.SemaphoreType.DMA((2, 4)), pltpu.SemaphoreType.DMA((2, 4))]
    adam = sum(job.count for job in jobs.values()) * TILE['up'][0] * D_FF
    rows = CORE_TILES * ROW_TILE if plan.rows else 0
    results = pl.pallas_call(
        functools.partial(fused_kernel, plan),
        grid_spec=pltpu.PrefetchScalarGridSpec(num_scalar_prefetch=1, grid=(plan.steps,), in_specs=in_specs, out_specs=out_specs, scratch_shapes=scratch),
        out_shape=out_shape,
        input_output_aliases=aliases,
        cost_estimate=pl.CostEstimate(flops=4 * rows * D_MODEL * D_FF + 2000 * adam, bytes_accessed=30 * adam + 4 * rows * D_MODEL, transcendentals=0),
        compiler_params=pltpu.CompilerParams(vmem_limit_bytes=58 * 1024 * 1024),
        name=name,
    )(place, *args)
    acts, results = results[:plan.n_act], results[plan.n_act:]
    n = len(plan.kinds)
    made = {kind: list(results[3 * i:3 * i + 3]) + ([results[3 * n + i]] if fresh else [None]) for i, kind in enumerate(plan.kinds)}
    return acts, made


def solution(mesh):
    replicas = mesh.shape['data']
    down_hop, up_hop, swap = [(1, 0)], [(0, 1)], [(0, 1), (1, 0)]
    w_spec = P(None, 'stage', None, None)
    g_spec = P('data', None, 'stage', None, None)
    s_spec = P(None, 'stage', 'data', None)
    dy_spec = P('data', None)
    x_spec = P(None, 'data', None)
    n_spec = P(None)

    def sharded(w_up, w_down, m_up, m_down, v_up, v_down, g_up, g_down, act_stash, dy_last, x_next, max_norm):
        pos = lax.axis_index('stage')
        rep = lax.axis_index('data')
        place = jnp.stack([pos, rep]).astype(jnp.int32)

        def backward(v, grad_top, late):
            f_up, f_down = w_up[v, 0], w_down[v, 0]
            if late is not None:
                f_up, f_down, _ = lax.optimization_barrier((f_up, f_down, late))
            old_up, old_down, stash = f_up.astype(BF16), f_down.astype(BF16), act_stash[v, 0]
            pre_act = jnp.dot(stash, old_up, preferred_element_type=F32)
            hidden = gelu_tanh(pre_act).astype(BF16)

            def chain(grad_y):
                d_hid = lax.dot_general(grad_y, old_down, CONTRACT_LAST, preferred_element_type=F32)
                d_pre = jax.vjp(gelu_tanh, pre_act)[1](d_hid)[0].astype(BF16)
                back_rows = lax.dot_general(d_pre, old_up, CONTRACT_LAST, preferred_element_type=F32)
                return d_pre, (grad_y.astype(F32) + back_rows).astype(BF16)

            zeros = (jnp.zeros(hidden.shape, BF16), jnp.zeros(grad_top.shape, BF16))
            first = lax.cond(pos == 1, chain, lambda g: zeros, grad_top)
            grad_mid = lax.ppermute(first[1], 'stage', down_hop)
            grad_y = jnp.where(pos == 1, grad_top, grad_mid)
            sum_down = lax.dot_general(hidden, grad_y, CONTRACT_ROWS, preferred_element_type=F32) + g_down[0, v, 0]
            part_down = lax.psum_scatter(sum_down, 'data', scatter_dimension=0, tiled=True)
            grad_mid, sum_down = lax.optimization_barrier((grad_mid, sum_down))
            d_pre, grad_bottom = lax.cond(pos == 0, chain, lambda g: first, grad_mid)
            sum_up = lax.dot_general(stash, d_pre, CONTRACT_ROWS, preferred_element_type=F32) + g_up[0, v, 0]
            part_up = lax.psum_scatter(sum_up, 'data', scatter_dimension=0, tiled=True)
            return lax.ppermute(grad_bottom, 'stage', up_hop), part_up, part_down, sum_down[:8, :128]

        grad_flow, up1, down1, late = backward(1, dy_last, None)
        grad_flow, up0, down0, _ = backward(0, grad_flow, late)
        up = [up0 / replicas, up1 / replicas]
        down = [down0 / replicas, down1 / replicas]

        part_sq = sum(jnp.sum(t * t) for t in up + down)
        total_sq = lax.psum(part_sq, ('data', 'stage'))
        clip = jnp.minimum(1.0, max_norm / (jnp.sqrt(total_sq) + 1e-6))

        def gather(t):
            return lax.all_gather(t, 'data', axis=0, tiled=True)

        state = {'up': (w_up, m_up, v_up), 'down': (w_down, m_down, v_down)}
        call = functools.partial(fused_call, place=place, clip=clip, state=state)
        n_micro, rows, width = x_next.shape
        half = n_micro // 2

        _, made = call('adam_own0', jobs={k: Job(k, 0, True) for k in state}, grads={'up': up[0], 'down': down[0]}, prev={}, fresh='own')
        fresh_up, fresh_down = gather(made['up'][3]), gather(made['down'][3])
        full_down1, full_up1, full_down0, full_up0 = gather(down[1]), gather(up[1]), gather(down[0]), gather(up[0])
        pair = (fresh_up, lax.ppermute(fresh_up, 'stage', swap), fresh_down, lax.ppermute(fresh_down, 'stage', swap))

        made = {k: made[k][:3] + [None] for k in made}
        (act,), made = call('fwd0', jobs={k: Job(k, 1, True) for k in state}, grads={'up': up[1], 'down': down[1]}, prev=made, fresh='all',
                            act=x_next.reshape(n_micro * rows, width), weights=pair, owner=0, first=True)
        (act,), more = call('fwd1', jobs={'down': Job('down', 1, False)}, grads={'down': full_down1}, prev=made, fresh='all', act=act, weights=pair, owner=1)
        made.update(more)
        _, more = call('adam_up1', jobs={'up': Job('up', 1, False)}, grads={'up': full_up1}, prev=made, fresh='all')
        made.update(more)
        fresh_up, fresh_down = made['up'][3], made['down'][3]
        pair = (fresh_up, lax.ppermute(fresh_up, 'stage', swap), fresh_down, lax.ppermute(fresh_down, 'stage', swap))
        (act,), _ = call('fwd2', jobs={}, grads={}, prev={}, fresh=None, act=act, weights=pair, owner=0)
        (own, y_next), more = call('fwd3', jobs={'down': Job('down', 0, False)}, grads={'down': full_down0}, prev=made, fresh=None, act=act, weights=pair, owner=1, last=True)
        made.update(more)
        other = lax.ppermute(own, 'stage', swap)
        _, more = call('adam_up0', jobs={'up': Job('up', 0, False)}, grads={'up': full_up0}, prev=made, fresh=None)
        made.update(more)
        y_next = lax.dynamic_update_slice_in_dim(y_next, other, (1 - pos) * half * rows, 0).reshape(n_micro, rows, width)
        up_new, down_new = made['up'], made['down']
        return (up_new[0], down_new[0], up_new[1], down_new[1], up_new[2], down_new[2], y_next)

    return jax.shard_map(sharded, mesh=mesh, in_specs=(w_spec, w_spec, w_spec, w_spec, w_spec, w_spec, g_spec, g_spec, s_spec, dy_spec, x_spec, n_spec), out_specs=(w_spec, w_spec, w_spec, w_spec, w_spec, w_spec, x_spec), check_vma=False)
```

time: 1700 us -> 1640 us (0.965)
  matrix products: 696 us -> 138 us
  Pallas kernels: 180 us -> 632 us
  waiting for transfers between devices: 595 us -> 737 us
  local copies, waits for them, and re-layouts: 114 us -> 53.9 us
  other arithmetic: 62.6 us -> 24 us
    dot_general x15 -> x7, matrix products: 660 us -> 103 us  [the longest x2 38 us: chain(): lax.dot_general(grad_y, old_down, CONTRACT_LAST, preferred_element_type=F32)]
    pallas_call x4 -> x7, Pallas kernels: 180 us -> 632 us  [fused_call(): pl.pallas_call(functools.partial(fused_kernel, plan), grid_spec=pltpu.Pre...]
    slice x6 -> x0, local copies, waits for them, and re-layouts: 71.2 us -> none  [the longest x4 47.4 us: shard(): return lax.dynamic_slice_in_dim(t[0, 0], rep * rows, rows, 0)]
    all_gather x6, waiting for transfers between devices: 109 us -> 175 us  [gather(): return lax.all_gather(t, 'data', axis=0, tiled=True)]
    reduce_scatter x2, waiting for transfers between devices: 147 us -> 203 us  [backward(): part_up = lax.psum_scatter(sum_up, 'data', scatter_dimension=0, tiled=True)]
    squeeze x0 -> x2, local copies, waits for them, and re-layouts: none -> 36.1 us  [backward(): f_up, f_down = (w_up[v, 0], w_down[v, 0])]
    ppermute x5, waiting for transfers between devices: 0.01 us -> 25.8 us  [the longest x2 13.1 us: sharded(): lax.ppermute(fresh_up, 'stage', swap)]
    select_n x1 -> x0, other arithmetic: 24.6 us -> none  [sharded(): jnp.where(pos == 0, jnp.concatenate([own, other]), jnp.concatenate([other...]
  transfers between devices with their start and end apart: 18 -> 18, of which waited for: 8 -> 12; matrix products, arithmetic and copies ran while one was open for 44% -> 5% of each run, Pallas kernels for 11% -> 37%
where the time goes in v3:
time: 1640 us
  waiting for transfers between devices  737 us (45%)
  Pallas kernels  632 us (39%)
  matrix products  138 us (8%)
  local copies, waits for them, and re-layouts  53.9 us (3%)
  other arithmetic  24 us (1%)
  blocking collectives  22.2 us (1%)
  between operations  18.6 us (1%)
    pallas_call x7, Pallas kernels, fused_call(): pl.pallas_call(functools.partial(fused_kernel, plan), grid_spec=pltpu.Pre...  632 us
    reduce_scatter x2, waiting for transfers between devices, backward(): lax.psum_scatter(sum_down, 'data', scatter_dimension=0, tiled=True)  290 us
    reduce_scatter x2, waiting for transfers between devices, backward(): part_up = lax.psum_scatter(sum_up, 'data', scatter_dimension=0, tiled=True)  203 us
    all_gather x6, waiting for transfers between devices, gather(): return lax.all_gather(t, 'data', axis=0, tiled=True)  175 us
    ppermute x2, waiting for transfers between devices, backward(): grad_mid = lax.ppermute(first[1], 'stage', down_hop)  39.7 us
    dot_general x2, matrix products, chain(): lax.dot_general(grad_y, old_down, CONTRACT_LAST, preferred_element_type=F32)  38 us
    squeeze x2, local copies, waits for them, and re-layouts, backward(): f_up, f_down = (w_up[v, 0], w_down[v, 0])  36.1 us
    dot_general x2, matrix products, backward(): lax.dot_general(hidden, grad_y, CONTRACT_ROWS, preferred_element_type=F32)  35.8 us
  transfers between devices with their start and end apart: 18, of which 12 were waited for; matrix products, arithmetic and copies ran while one was open for 5% of the time, Pallas kernels for 37%

profile of v3, /device:TPU:0, one launch (start us, length us, event | category | flops | bytes accessed | tf_op | source)
XLA Modules:
  0.0 1640.0 jit_solution(9235508353924604732)
XLA Ops:
  7.2 0.0 reduce-scatter.7.cloned.1.call-start
  7.2 18.0 %slice_bitcast_fusion.1 = (bf16[1024,4096]{1,0:T(8,128)(2,1)}, bf16[1024,4096]{1,0:T(8,128)(2,1)}) fusion(f32[2,1,1024,4096]{3,2,1,0:T(8,128)} %refs_1_.5), kind=kLoop, calls=%fused_computation.47 | loop fusion | bytes 33554432 | tf_op jit(solution)/shard_map/squeeze | solution.py:241
  25.2 18.1 %slice_bitcast_fusion = (bf16[4096,1024]{1,0:T(8,128)(2,1)}, bf16[4096,1024]{1,0:T(8,128)(2,1)}) fusion(f32[2,1,4096,1024]{3,2,1,0:T(8,128)} %refs_6_.7), kind=kLoop, calls=%fused_computation.46 | loop fusion | bytes 33554432 | tf_op jit(solution)/shard_map/squeeze | solution.py:241
  43.3 12.6 fusion.59
  55.9 4.2 conditional.4
  55.9 3.5 broadcast.68
  59.4 0.2 broadcast.69
  60.1 7.5 collective-permute-start
  67.6 22.3 %collective-permute-done = bf16[768,1024]{1,0:T(8,128)(2,1)S(1)} collective-permute-done((bf16[768,1024]{1,0:T(8,128)(2,1)S(1)}, bf16[768,1024]{1,0:T(8,128)(2,1)S(1)}, u32[]{:S(2)}, u32[]{:S(2)}) %collective-permute-start) | collective-permute-done | bytes 1572896 | tf_op jit(solution)/shard_map/ppermute | solution.py:256
  89.9 17.7 %bitcast_add_fusion.3 = f32[4096,1024]{1,0:T(8,128)} fusion(f32[1,2,1,4096,1024]{4,3,2,1,0:T(8,128)} %param.27, f32[768,4096]{1,0:T(8,128)} %fusion.59, bf16[768,1024]{1,0:T(8,128)(2,1)} %param.29, bf16[768,1024]{1,0:T(8,128)(2,1)S(1)} %collective-permute-done, pred[]{:T(512)S(6)} %eq.5), kind=kOutput, calls=%fused_computation.45 | convolution fusion | flops 6475743232 | bytes 49283072 | tf_op jit(solution)/shard_map/dot_general | solution.py:258
  107.5 27.4 %conditional.5 = ((bf16[768,4096]{1,0:T(8,128)(2,1)}, bf16[768,1024]{1,0:T(8,128)(2,1)S(1)})) conditional(s32[]{:T(128)} %convert_element_type.61, (bf16[768,4096]{1,0:T(8,128)(2,1)}, bf16[768,1024]{1,0:T(8,128)(2,1)S(1)}) %conditional.4, (bf16[768,1024]{1,0:T(8,128)(2,1)S(1)}, bf16[4096,1024]{1,0:T(8,128)(2,1)}, f32[768,4096]{1,0:T(8,128)}, ...), branch_computations={%region_2.3_spmd, %region_3.4_spmd} | conditional | flops 12950175744 | bytes 80216120 | solution.py:261
  107.5 18.4 %fusion.13 = bf16[768,4096]{1,0:T(8,128)(2,1)} fusion(f32[768,4096]{1,0:T(8,128)} %get-tuple-element.45, bf16[768,1024]{1,0:T(8,128)(2,1)S(1)} %get-tuple-element.43, bf16[4096,1024]{1,0:T(8,128)(2,1)} %get-tuple-element.44), kind=kOutput, calls=%fused_computation.18 | convolution fusion | flops 6505365504 | bytes 28835840 | tf_op jit(solution)/shard_map/cond/branch_1_fun/dot_general | solution.py:249
  125.9 8.8 add_convert_fusion.1
  134.9 15.2 bitcast_add_fusion
  150.1 0.0 reduce-scatter.11.cloned.1.call-start
  150.2 0.7 reduce-scatter.11.cloned.1.call-update
  150.9 0.0 reduce-scatter.5.cloned.1.call-start
  150.9 1.4 collective-permute-start.1
  152.3 12.2 convolution_bitcast_fusion
  164.6 4.1 conditional.6
  164.6 3.5 broadcast.81
  168.0 0.2 broadcast.80
  168.6 1.3 collective-permute-start.2
  169.9 17.4 %collective-permute-done.2 = bf16[768,1024]{1,0:T(8,128)(2,1)} collective-permute-done((bf16[768,1024]{1,0:T(8,128)(2,1)S(1)}, bf16[768,1024]{1,0:T(8,128)(2,1)}, u32[]{:S(2)}, u32[]{:S(2)}) %collective-permute-start.2) | collective-permute-done | bytes 1572896 | tf_op jit(solution)/shard_map/ppermute | solution.py:256
  187.3 18.1 %bitcast_add_fusion.2 = f32[4096,1024]{1,0:T(8,128)} fusion(f32[1,2,1,4096,1024]{4,3,2,1,0:T(8,128)} %param.27, f32[768,4096]{1,0:T(8,128)} %convolution_bitcast_fusion, bf16[768,1024]{1,0:T(8,128)(2,1)S(1)} %collective-permute-done.1, bf16[768,1024]{1,0:T(8,128)(2,1)} %collective-permute-done.2, pred[]{:T(512)S(6)} %eq.5), kind=kOutput, calls=%fused_computation.44 | convolution fusion | flops 6475743232 | bytes 49283072 | tf_op jit(solution)/shard_map/dot_general | solution.py:258
  205.4 19.8 %conditional.7 = (bf16[768,4096]{1,0:T(8,128)(2,1)}) conditional(s32[]{:T(128)} %convert_element_type.61, bf16[768,4096]{1,0:T(8,128)(2,1)} %get-tuple-element.109, (bf16[768,1024]{1,0:T(8,128)(2,1)}, bf16[4096,1024]{1,0:T(8,128)(2,1)}, f32[768,4096]{1,0:T(8,128)}) %tuple.52), branch_computations={%region_6.7_spmd, %region_7.8_spmd} | conditional | flops 6505365504 | bytes 28835848 | solution.py:261
  205.6 19.7 %fusion.27 = bf16[768,4096]{1,0:T(8,128)(2,1)} fusion(f32[768,4096]{1,0:T(8,128)} %get-tuple-element.53, bf16[768,1024]{1,0:T(8,128)(2,1)} %get-tuple-element.51, bf16[4096,1024]{1,0:T(8,128)(2,1)} %get-tuple-element.52), kind=kOutput, calls=%fused_computation.38 | convolution fusion | flops 6505365504 | bytes 28835840 | tf_op jit(solution)/shard_map/cond/branch_1_fun/dot_general | solution.py:249
  225.2 15.7 bitcast_add_fusion.1
  240.9 0.0 reduce-scatter.9.cloned.1.call-start
  241.0 0.5 reduce-scatter.9.cloned.1.call-update
  241.5 0.3 all-gather.11.cloned.1.call-start
  241.8 0.6 pad_add_fusion.place
  242.3 57.7 %reduce-scatter.7.cloned.1.call-done = f32[256,4096]{1,0:T(8,128)} async-done(((f32[1024,4096]{1,0:T(8,128)}), f32[256,4096]{1,0:T(8,128)}) %reduce-scatter.7.cloned.1.call-update) | async-done | bytes 4194320 | tf_op jit(solution)/shard_map/reduce_scatter | solution.py:263
  300.1 5.8 broadcast_multiply_fusion.2
  305.9 145.8 %reduce-scatter.11.cloned.1.call-done = f32[1024,1024]{1,0:T(8,128)} async-done(((f32[4096,1024]{1,0:T(8,128)}), f32[1024,1024]{1,0:T(8,128)}) %reduce-scatter.11.cloned.1.call-update) | async-done | bytes 4194320 | tf_op jit(solution)/shard_map/reduce_scatter | solution.py:259
  451.6 5.9 broadcast_multiply_fusion
  457.5 145.7 %reduce-scatter.5.cloned.1.call-done = f32[256,4096]{1,0:T(8,128)} async-done(((f32[1024,4096]{1,0:T(8,128)}), f32[256,4096]{1,0:T(8,128)}) %reduce-scatter.5.cloned.1.call-update) | async-done | bytes 4194320 | tf_op jit(solution)/shard_map/reduce_scatter | solution.py:263
  603.2 5.8 broadcast_multiply_fusion.3
  610.3 144.3 %reduce-scatter.9.cloned.1.call-done = f32[1024,1024]{1,0:T(8,128)} async-done(((f32[4096,1024]{1,0:T(8,128)}), f32[1024,1024]{1,0:T(8,128)}) %reduce-scatter.9.cloned.1.call-update) | async-done | bytes 4194320 | tf_op jit(solution)/shard_map/reduce_scatter | solution.py:259
  754.6 5.9 broadcast_multiply_fusion.1
  762.5 22.2 %psum.7 = f32[]{:T(128)} all-reduce(f32[]{:T(128)S(6)} %add.96), channel_id=1, replica_groups=mesh['data'=4,'stage'=2] {'data','stage'}, use_global_device_ids=true, to_apply=%region_16.17 | all-reduce | flops 1 | bytes 8 | tf_op jit(solution)/shard_map/psum | solution.py:272
  785.5 22.0 %adam_own0.1 = (f32[2,1,1024,4096]{3,2,1,0:T(8,128)}, f32[2,1,1024,4096]{3,2,1,0:T(8,128)}, f32[2,1,1024,4096]{3,2,1,0:T(8,128)}, f32[2,1,4096,1024]{3,2,1,0:T(8...) custom-call(s32[2]{0:T(128)} %pad_add_fusion.place, ...), custom_call_target="tpu_custom_call" | custom-call | flops 4194304000 | bytes 62914560 | tf_op jit(solution)/shard_map/adam_own0/pallas_call | solution.py:210
  807.5 0.0 all-gather.13.cloned.1.call-start
  807.5 0.5 all-gather.13.cloned.1.call-update
  808.1 0.0 all-gather.15.cloned.1.call-start
  808.1 0.7 all-gather.15.cloned.1.call-update
  808.8 0.0 all-gather.9.cloned.1.call-start
  808.9 0.7 all-gather.9.cloned.1.call-update
  809.6 0.0 all-gather.17.cloned.1.call-start
  809.6 81.7 %all-gather.11.cloned.1.call-done.refs_2_ = bf16[1024,4096]{1,0:T(8,128)(2,1)} async-done(((bf16[256,4096]{1,0:T(8,128)(2,1)}), bf16[1024,4096]{1,0:T(8,128)(2,1)}) %all-gather.11.cloned.1.call-update) | async-done | bytes 8388624 | tf_op jit(solution)/shard_map/all_gather | solution.py:276
  891.4 83.5 %all-gather.13.cloned.1.call-done.refs_4_ = bf16[4096,1024]{1,0:T(8,128)(2,1)} async-done(((bf16[1024,1024]{1,0:T(8,128)(2,1)}), bf16[4096,1024]{1,0:T(8,128)(2,1)}) %all-gather.13.cloned.1.call-update) | async-done | bytes 8388624 | tf_op jit(solution)/shard_map/all_gather | solution.py:276
  974.9 0.3 all-gather.7.cloned.1.call-start
  975.2 12.8 collective-permute-done.4.refs_5_
  988.0 152.0 %fwd0.1 = (bf16[6144,1024]{1,0:T(8,128)(2,1)}, f32[2,1,1024,4096]{3,2,1,0:T(8,128)}, f32[2,1,1024,4096]{3,2,1,0:T(8,128)}, f32[2,1,1024,4096]{3,2,1,0:T(8,128)},...) custom-call(s32[2]{0:T(128)} %pad_add_fusion.place, ...), custom_call_target="tpu_custom_call", output_to_operand_aliasing={{1}: (15, {}), {2}: (16, {}), {3}: (17, {}), {4}: (18, {}),... | custom-call | flops 107273519104 | bytes 88080384 | tf_op jit(solution)/shard_map/fwd0/pallas_call | solution.py:210
  1140.0 136.1 %fwd1.1 = (bf16[6144,1024]{1,0:T(8,128)(2,1)}, f32[2,1,4096,1024]{3,2,1,0:T(8,128)}, f32[2,1,4096,1024]{3,2,1,0:T(8,128)}, f32[2,1,4096,1024]{3,2,1,0:T(8,128)}, bf16[4096,1024]{1,0:T(8,128)(2,1)}) custom-call(s32[2]{0:T(128)} %pad_add_fusion.place, f32[1]{0:T(128)S(6)} %min.3.refs_0_, ...), custom_call_target="tpu_custom_call", output_to_operand_aliasing={{1}: (11, {}), {2}: (12, {}), {3}: (13, {}), {4}: (14, {})} | custom-call | flops 109370671104 | bytes 119537664 | tf_op jit(solution)/shard_map/fwd1/pallas_call | solution.py:210
  1276.1 0.8 collective-permute-start.6
  1276.9 5.3 all-gather.9.cloned.1.call-done.refs_4_
  1282.1 35.1 %adam_up1.1 = (f32[2,1,1024,4096]{3,2,1,0:T(8,128)}, f32[2,1,1024,4096]{3,2,1,0:T(8,128)}, f32[2,1,1024,4096]{3,2,1,0:T(8,128)}, bf16[1024,4096]{1,0:T(8,128)(2,1)}) custom-call(s32[2]{0:T(128)} %pad_add_fusion.place, f32[1]{0:T(128)S(6)} %min.3.refs_0_, ...), custom_call_target="tpu_custom_call", output_to_operand_aliasing={{0}: (6, {}), {1}: (7, {}), {2}: (8, {}), {3}: (9, {})} | custom-call | flops 6291456000 | bytes 94371840 | tf_op jit(solution)/shard_map/adam_up1/pallas_call | solution.py:210
  1317.3 13.1 collective-permute-done.5.refs_3_
  1330.4 118.9 %fwd2.1.refs_1_ = bf16[6144,1024]{1,0:T(8,128)(2,1)} custom-call(s32[2]{0:T(128)} %pad_add_fusion.place, f32[1]{0:T(128)S(6)} %min.3.refs_0_, bf16[6144,1024]{1,0:T(8,128)(2,1)} %get-tuple-element.134.refs_1_, bf16[1024,4096]{1,0:T(8,128)(2,1)} %get-tuple-element.135.refs_2_, bf16[1024,4096]{1,0:T(8,128)(2,1)} %collective-permute-done.5.refs_3_, ...), custom_call_target="tpu_custom_call" | custom-call | flops 103079215104 | bytes 25165824 | tf_op jit(solution)/shard_map/fwd2/pallas_call | solution.py:210
  1449.4 135.3 %fwd3.1 = (bf16[6144,1024]{1,0:T(8,128)(2,1)}, bf16[12288,1024]{1,0:T(8,128)(2,1)}, f32[2,1,4096,1024]{3,2,1,0:T(8,128)}, f32[2,1,4096,1024]{3,2,1,0:T(8,128)}, f32[2,1,4096,1024]{3,2,1,0:T(8,128)}) custom-call(s32[2]{0:T(128)} %pad_add_fusion.place, f32[1]{0:T(128)S(6)} %min.3.refs_0_, ...), custom_call_target="tpu_custom_call", output_to_operand_aliasing={{2}: (11, {}), {3}: (12, {}), {4}: (13, {})} | custom-call | flops 109370671104 | bytes 119537664 | tf_op jit(solution)/shard_map/fwd3/pallas_call | solution.py:210
  1584.7 4.6 all-gather.7.cloned.1.call-done.refs_4_
  1589.3 33.0 %adam_up0.1 = (f32[2,1,1024,4096]{3,2,1,0:T(8,128)}, f32[2,1,1024,4096]{3,2,1,0:T(8,128)}, f32[2,1,1024,4096]{3,2,1,0:T(8,128)}) custom-call(s32[2]{0:T(128)} %pad_add_fusion.place, f32[1]{0:T(128)S(6)} %min.3.refs_0_, f32[2,1,1024,4096]{3,2,1,0:T(8,128)} %refs_1_.5, ...), custom_call_target="tpu_custom_call", output_to_operand_aliasing={{0}: (6, {}), {1}: (7, {}), {2}: (8, {})} | custom-call | flops 6291456000 | bytes 94371840 | tf_op jit(solution)/shard_map/adam_up0/pallas_call | solution.py:210
  1622.4 10.5 constant_dynamic-update-slice_fusion
  (23 shorter events, 0.2 us)
Async XLA Ops:
  7.2 292.9 %reduce-scatter.7.cloned.1.call-start = ((), (), s32[]{:S(2)}) async-start(), calls=%async_computation.5 | async-start | bytes 20971520 | tf_op jit(solution)/shard_map/reduce_scatter | solution.py:263
  25.2 18.1 %copy-start.3 = (bf16[2,1,768,1024]{3,2,1,0:T(8,128)(2,1)S(1)}, bf16[2,1,768,1024]{3,2,1,0:T(8,128)(2,1)}, u32[]{:S(2)}) copy-start(bf16[2,1,768,1024]{3,2,1,0:T(8,128)(2,1)} %param.28) | copy-start | bytes 9437188
  43.3 12.6 copy-start.1
  60.1 29.8 %collective-permute-start = (bf16[768,1024]{1,0:T(8,128)(2,1)S(1)}, bf16[768,1024]{1,0:T(8,128)(2,1)S(1)}, u32[]{:S(2)}, u32[]{:S(2)}) collective-permute-start(bf16[768,1024]{1,0:T(8,128)(2,1)S(1)} %get-tuple-element.104), channel_id=1, source_target_pairs={{1,0},{3,2},{5,4},{7,6}} | collective-permute-start | bytes 4718600 | tf_op jit(solution)/shard_map/ppermute | solution.py:256
  107.5 18.4 %copy-start.2 = (bf16[1024,4096]{1,0:T(8,128)(2,1)S(1)}, bf16[1024,4096]{1,0:T(8,128)(2,1)}, u32[]{:S(2)}) copy-start(bf16[1024,4096]{1,0:T(8,128)(2,1)} %get-tuple-element.46) | copy-start | bytes 25165828 | tf_op jit(solution)/shard_map/cond
  150.1 301.5 %reduce-scatter.11.cloned.1.call-start = ((), (), s32[]{:S(2)}) async-start(), calls=%async_computation.7 | async-start | bytes 20971520 | tf_op jit(solution)/shard_map/reduce_scatter | solution.py:259
  150.9 452.3 %reduce-scatter.5.cloned.1.call-start = ((), (), s32[]{:S(2)}) async-start(), calls=%async_computation.4 | async-start | bytes 20971520 | tf_op jit(solution)/shard_map/reduce_scatter | solution.py:263
  150.9 13.6 collective-permute-start.1
  168.6 18.7 %collective-permute-start.2 = (bf16[768,1024]{1,0:T(8,128)(2,1)S(1)}, bf16[768,1024]{1,0:T(8,128)(2,1)}, u32[]{:S(2)}, u32[]{:S(2)}) collective-permute-start(bf16[768,1024]{1,0:T(8,128)(2,1)S(1)} %get-tuple-element.110), channel_id=1, source_target_pairs={{1,0},{3,2},{5,4},{7,6}} | collective-permute-start | bytes 4718600 | tf_op jit(solution)/shard_map/ppermute | solution.py:256
  205.4 19.8 %copy-start.4 = (bf16[2,1,768,1024]{3,2,1,0:T(8,128)(2,1)S(1)}, bf16[2,1,768,1024]{3,2,1,0:T(8,128)(2,1)}, u32[]{:S(2)}) copy-start(bf16[2,1,768,1024]{3,2,1,0:T(8,128)(2,1)} %param.28) | copy-start | bytes 9437188
  240.9 513.7 %reduce-scatter.9.cloned.1.call-start = ((), (), s32[]{:S(2)}) async-start(), calls=%async_computation.6 | async-start | bytes 20971520 | tf_op jit(solution)/shard_map/reduce_scatter | solution.py:259
  241.5 649.8 %all-gather.11.cloned.1.call-start = ((), (), s32[]{:S(2)}) async-start(), calls=%async_computation.10 | async-start | bytes 10485760 | tf_op jit(solution)/shard_map/all_gather | solution.py:276
  807.5 167.4 %all-gather.13.cloned.1.call-start = ((), (), s32[]{:S(2)}) async-start(), calls=%async_computation.11 | async-start | bytes 10485760 | tf_op jit(solution)/shard_map/all_gather | solution.py:276
  808.1 331.9 %all-gather.15.cloned.1.call-start = ((), (), s32[]{:S(2)}) async-start(), calls=%async_computation.12 | async-start | bytes 20971520 | tf_op jit(solution)/shard_map/all_gather | solution.py:276
  808.8 473.3 %all-gather.9.cloned.1.call-start = ((), (), s32[]{:S(2)}) async-start(), calls=%async_computation.9 | async-start | bytes 20971520 | tf_op jit(solution)/shard_map/all_gather | solution.py:276
  809.6 639.8 %all-gather.17.cloned.1.call-start = ((), (), s32[]{:S(2)}) async-start(), calls=%async_computation.13 | async-start | bytes 20971520 | tf_op jit(solution)/shard_map/all_gather | solution.py:276
  891.4 83.8 %collective-permute-start.3 = (bf16[1024,4096]{1,0:T(8,128)(2,1)}, bf16[1024,4096]{1,0:T(8,128)(2,1)}, u32[]{:S(2)}, u32[]{:S(2)}) collective-permute-start(bf16[1024,4096]{1,0:T(8,128)(2,1)} %all-gather.11.cloned.1.call-done.refs_2_), channel_id=1, source_target_pairs={{0,1},{1,0},{2,3},{3,2},{4,5},{5,4},{6,7},{7,6}} | collective-permute-start | bytes 25165832 | tf_op jit(solution)/shard_map/ppermute | solution.py:286
  974.9 13.1 collective-permute-start.4
  974.9 614.4 %all-gather.7.cloned.1.call-start = ((), (), s32[]{:S(2)}) async-start(), calls=%async_computation.8 | async-start | bytes 20971520 | tf_op jit(solution)/shard_map/all_gather | solution.py:276
  1276.1 41.3 %collective-permute-start.6 = (bf16[4096,1024]{1,0:T(8,128)(2,1)}, bf16[4096,1024]{1,0:T(8,128)(2,1)}, u32[]{:S(2)}, u32[]{:S(2)}) collective-permute-start(bf16[4096,1024]{1,0:T(8,128)(2,1)} %get-tuple-element.136.refs_4_), channel_id=1, source_target_pairs={{0,1},{1,0},{2,3},{3,2},{4,5},{5,4},{6,7},{7,6}} | collective-permute-start | bytes 25165832 | tf_op jit(solution)/shard_map/ppermute | solution.py:296
  1317.3 13.1 collective-permute-start.5
  1584.6 37.7 %collective-permute-start.7 = (bf16[6144,1024]{1,0:T(8,128)(2,1)}, bf16[6144,1024]{1,0:T(8,128)(2,1)}, u32[]{:S(2)}, u32[]{:S(2)}) collective-permute-start(bf16[6144,1024]{1,0:T(8,128)(2,1)} %get-tuple-element.146), channel_id=1, source_target_pairs={{0,1},{1,0},{2,3},{3,2},{4,5},{5,4},{6,7},{7,6}} | collective-permute-start | bytes 37748744 | tf_op jit(solution)/shard_map/ppermute | solution.py:300
Sparse Core Ops, SparseCore 0:
  150.2 149.7 reduce-scatter.6
  303.6 147.9 reduce-scatter.10
  455.2 147.9 reduce-scatter.4
  606.6 147.9 reduce-scatter.8
  807.6 83.7 all-gather.10
  893.0 81.8 all-gather.12
  976.6 151.8 all-gather.14
  1130.3 151.8 all-gather.8
  1283.9 151.8 all-gather.16
  1437.4 151.8 all-gather.6
